TPU v7x, 32 devices: a whole 2x2x4 slice. The times are simulated.
32 devices in a mesh: seq: 8 (over y, x, core), fsdp: 4 (over z).
Axes of the slice: x: 2, y: 2, z: 4, core: 2. Of those that a mesh axis runs over, the one named last changes fastest.
Arguments:
- stream: float32 [4, 1024, 2048], P('fsdp', 'seq'), may hold values from -6 to 6
- segments: int32 [4, 1024], P('fsdp'), may hold values from 0 to 3, never falling along the last dimension, each value on 1 to 512 neighbouring positions
- attention_weights: float32 [2048, 8192], P(('seq', 'fsdp')), may hold values from -4 to 4
- feedforward_weights: float32 [2048, 16896], P(('seq', 'fsdp')), may hold values from -4 to 4
- norm_vectors: float32 [7, 2048], P(None, ('seq', 'fsdp')), may hold values from -2 to 2
- attention_moments: float32 [2, 2048, 8192], P(None, ('seq', 'fsdp')), may hold values from -1 to 1, as said below
- feedforward_moments: float32 [2, 2048, 16896], P(None, ('seq', 'fsdp')), may hold values from -1 to 1, as said below
- vector_moments: float32 [2, 7, 2048], P(None, None, ('seq', 'fsdp')), may hold values from -1 to 1, as said below
- cotangent: float32 [4, 1024, 2048], P('fsdp', 'seq'), may hold values from -1 to 1
Outputs:
- output_stream: float32 [4, 1024, 2048], P('fsdp', 'seq')
- stream_grad: float32 [4, 1024, 2048], P('fsdp', 'seq')
- attention_grad: float32 [2048, 8192], P(('seq', 'fsdp'))
- feedforward_grad: float32 [2048, 16896], P(('seq', 'fsdp'))
- vector_grad: float32 [7, 2048], P(None, ('seq', 'fsdp'))
- attention_new: float32 [2048, 8192], P(('seq', 'fsdp'))
- feedforward_new: float32 [2048, 16896], P(('seq', 'fsdp'))
- vector_new: float32 [7, 2048], P(None, ('seq', 'fsdp'))
- attention_state: float32 [2, 2048, 8192], P(None, ('seq', 'fsdp'))
- feedforward_state: float32 [2, 2048, 16896], P(None, ('seq', 'fsdp'))
- vector_state: float32 [2, 7, 2048], P(None, None, ('seq', 'fsdp'))
Inputs may be any that keep to these rules, and one draw needn't show every extreme that they name: `segments`: segment numbers never fall along a sequence; every one of the 4 documents is present. `attention_moments`: the second moments (index 1 of the first dimension) lie within 0.01 to 0.1. `feedforward_moments`: the second moments (index 1 of the first dimension) lie within 0.01 to 0.1. `vector_moments`: the second moments (index 1 of the first dimension) lie within 0.01 to 0.1.
All inputs are finite; a program needn't handle non-finite values.
Results may differ from a plain program's by a relative error of at most 0.025.
The roundings to bfloat16 on the way count: a program that leaves them out, or rounds other values in their place, can miss the bound.
Values may be sent and summed in bfloat16 or wider, within the bound.
A program may use at most 384 MiB of HBM per device.

v0:
```python
import jax
import jax.numpy as jnp
from jax import lax
from jax.sharding import PartitionSpec as P

D = 2048
H = 32
HD = 64
ROT = 16
FF = 5632


norm_epsilon = 1e-05
rope_base = 10000.0
neg_fill = -1e30
learn_rate = 0.01
beta_first = 0.9
beta_second = 0.95
adam_epsilon = 1e-08
decay_rate = 0.1
adam_step = 2.0


def document_positions(segment_ids):
    length = segment_ids.shape[0]
    indices = jnp.arange(length, dtype=jnp.int32)
    changes = jnp.concatenate(
        [jnp.ones((1,), dtype=jnp.bool_), segment_ids[1:] != segment_ids[:-1]]
    )
    starts = lax.cummax(jnp.where(changes, indices, jnp.zeros_like(indices)), axis=0)
    return indices - starts


def rotary_tables(positions, half_rot):
    powers = jnp.arange(half_rot, dtype=jnp.float32) / float(half_rot)
    inverse = rope_base ** (-powers)
    angles = positions.astype(jnp.float32)[:, None] * inverse[None, :]
    return (jnp.cos(angles), jnp.sin(angles))


def rotate(values, cosine, sine, half_rot, direction):
    first = values[..., :half_rot]
    second = values[..., half_rot : 2 * half_rot]
    cosine_wide = cosine[:, None, :]
    sine_wide = sine[:, None, :] * direction
    return jnp.concatenate(
        [
            first * cosine_wide - second * sine_wide,
            second * cosine_wide + first * sine_wide,
            values[..., 2 * half_rot :],
        ],
        axis=-1,
    )


def norm_forward(values, gain, shift):
    centred = values - jnp.mean(values, axis=-1, keepdims=True)
    inverse = lax.rsqrt(jnp.mean(centred * centred, axis=-1, keepdims=True) + norm_epsilon)
    normal_part = centred * inverse
    return (normal_part * gain + shift, normal_part, inverse)


def norm_backward(upstream, normal_part, inverse, gain):
    scaled = upstream * gain
    return inverse * (
        scaled
        - jnp.mean(scaled, axis=-1, keepdims=True)
        - normal_part * jnp.mean(scaled * normal_part, axis=-1, keepdims=True)
    )


def contract_rows(left, right):
    return lax.dot_general(
        left, right, (((0,), (0,)), ((), ())), preferred_element_type=jnp.float32
    )


def contract_cols(left, right):
    return lax.dot_general(
        left, right, (((1,), (1,)), ((), ())), preferred_element_type=jnp.float32
    )


def block_mask(segment_ids, start_row, block_rows):
    total_keys = segment_ids.shape[0]
    row_ids = start_row + jnp.arange(block_rows, dtype=jnp.int32)
    col_ids = jnp.arange(total_keys, dtype=jnp.int32)
    row_segments = lax.dynamic_slice_in_dim(segment_ids, start_row, block_rows)
    return (col_ids[None, :] <= row_ids[:, None]) & (segment_ids[None, :] == row_segments[:, None])


def adamw_update(weight, grad, moments, decay):
    first = beta_first * moments[0] + (1.0 - beta_first) * grad
    second = beta_second * moments[1] + (1.0 - beta_second) * grad * grad
    correct_one = 1.0 - beta_first**adam_step
    correct_two = 1.0 - beta_second**adam_step
    update = first / correct_one / (jnp.sqrt(second / correct_two) + adam_epsilon)
    return (weight - learn_rate * (update + decay * weight), jnp.stack([first, second]))


def body(
    stream,
    segments,
    attention_weights,
    feedforward_weights,
    norm_vectors,
    attention_moments,
    feedforward_moments,
    vector_moments,
    cotangent,
):
    groups = lax.axis_size("seq")
    shards = lax.axis_size("fsdp")
    my_rank = lax.axis_index("seq")
    tokens = stream.shape[1]
    length = tokens * groups
    local_heads = H // groups
    local_width = local_heads * HD
    unit_width = FF // groups
    owned_rows = D // (groups * shards)
    half_rot = ROT // 2
    score_scale = float(HD) ** (-0.5)
    block_rows = min(512, length)
    block_starts = jnp.arange(length // block_rows, dtype=jnp.int32) * block_rows
    attention_low, vector_low = (
        lax.all_gather(attention_weights.astype(jnp.bfloat16), ("seq", "fsdp"), axis=0, tiled=True),
        lax.all_gather(norm_vectors.astype(jnp.bfloat16), ("seq", "fsdp"), axis=1, tiled=True),
    )
    feedforward_low = lax.all_gather(
        feedforward_weights.astype(jnp.bfloat16), ("seq", "fsdp"), axis=0, tiled=True
    )
    vector_full = vector_low.astype(jnp.float32)
    gain_one, shift_one, bias_query, bias_key, bias_value, gain_two, shift_two = [
        vector_full[row_index] for row_index in range(7)
    ]
    segment_ids = segments[0]
    positions = document_positions(segment_ids)
    cosine_all, sine_all = rotary_tables(positions, half_rot)
    cosine = lax.dynamic_slice_in_dim(cosine_all, my_rank * tokens, tokens)
    sine = lax.dynamic_slice_in_dim(sine_all, my_rank * tokens, tokens)
    inputs = stream[0]
    normed_one, normal_one, inverse_one = norm_forward(inputs, gain_one, shift_one)
    normed_low = normed_one.astype(jnp.bfloat16)
    projected = jnp.dot(
        normed_low, attention_low[:, : 3 * D], preferred_element_type=jnp.float32
    ) + jnp.concatenate([bias_query, bias_key, bias_value])
    query_rot = rotate(projected[:, :D].reshape(tokens, H, HD), cosine, sine, half_rot, 1.0).astype(
        jnp.bfloat16
    )
    key_rot = rotate(
        projected[:, D : 2 * D].reshape(tokens, H, HD), cosine, sine, half_rot, 1.0
    ).astype(jnp.bfloat16)
    value_low = projected[:, 2 * D :].astype(jnp.bfloat16)
    packed = jnp.stack(
        [
            query_rot.reshape(tokens, groups, local_width),
            key_rot.reshape(tokens, groups, local_width),
            value_low.reshape(tokens, groups, local_width),
        ],
        axis=1,
    )
    by_head = lax.all_to_all(packed, "seq", split_axis=2, concat_axis=0, tiled=True)
    query_all = by_head[:, 0, 0].reshape(length, local_heads, HD)
    key_all = by_head[:, 1, 0].reshape(length, local_heads, HD)
    value_all = by_head[:, 2, 0].reshape(length, local_heads, HD)

    def forward_block(start_row):
        query_block = lax.dynamic_slice_in_dim(query_all, start_row, block_rows)
        scores = (
            jnp.einsum("bhd,lhd->hbl", query_block, key_all, preferred_element_type=jnp.float32)
            * score_scale
        )
        scores = jnp.where(block_mask(segment_ids, start_row, block_rows)[None], scores, neg_fill)
        row_max = jnp.max(scores, axis=-1, keepdims=True)
        weights_raw = jnp.exp(scores - row_max)
        row_sum = jnp.sum(weights_raw, axis=-1, keepdims=True)
        probability = (weights_raw / row_sum).astype(jnp.bfloat16)
        output_block = jnp.einsum(
            "hbl,lhd->bhd", probability, value_all, preferred_element_type=jnp.float32
        ).astype(jnp.bfloat16)
        return (output_block, (row_max + jnp.log(row_sum))[..., 0])

    output_blocks, logsum_blocks = lax.map(forward_block, block_starts)
    output_heads = output_blocks.reshape(length, local_heads, HD)
    attended = lax.all_to_all(
        output_heads.reshape(groups, tokens, local_width),
        "seq",
        split_axis=0,
        concat_axis=2,
        tiled=True,
    )[0]
    hidden = inputs + jnp.dot(
        attended, attention_low[:, 3 * D :], preferred_element_type=jnp.float32
    )
    normed_two, normal_two, inverse_two = norm_forward(hidden, gain_two, shift_two)
    normed_low_two = normed_two.astype(jnp.bfloat16)
    gate_up = jnp.dot(
        normed_low_two, feedforward_low[:, : 2 * FF], preferred_element_type=jnp.float32
    )
    gate_part = gate_up[:, :FF]
    up_part = gate_up[:, FF:]
    sigmoid_gate = jax.nn.sigmoid(gate_part)
    activated = (gate_part * sigmoid_gate * up_part).astype(jnp.bfloat16)
    result = hidden + contract_cols(activated, feedforward_low[:, 2 * FF :])
    feedforward_back = lax.all_gather(
        feedforward_weights.astype(jnp.bfloat16), ("seq", "fsdp"), axis=0, tiled=True
    )
    upstream = cotangent[0]
    cotangent_low = upstream.astype(jnp.bfloat16)
    grad_act = jnp.dot(
        cotangent_low, feedforward_back[:, 2 * FF :], preferred_element_type=jnp.float32
    )
    grad_gate = grad_act * up_part * sigmoid_gate * (1.0 + gate_part * (1.0 - sigmoid_gate))
    grad_up = grad_act * gate_part * sigmoid_gate
    grad_gate_up = jnp.concatenate([grad_gate, grad_up], axis=1).astype(jnp.bfloat16)
    grad_normed_two = contract_cols(grad_gate_up, feedforward_back[:, : 2 * FF])
    unit_stack = jnp.stack(
        [
            grad_gate_up[:, :FF].reshape(tokens, groups, unit_width),
            grad_gate_up[:, FF:].reshape(tokens, groups, unit_width),
            activated.reshape(tokens, groups, unit_width),
        ],
        axis=1,
    )
    unit_cols = lax.all_to_all(unit_stack, "seq", split_axis=2, concat_axis=0, tiled=True)[:, :, 0]
    normed_two_all, cotangent_all = (
        lax.all_gather(normed_low_two, "seq", axis=0, tiled=True),
        lax.all_gather(cotangent_low, "seq", axis=0, tiled=True),
    )
    feedforward_in_term = contract_rows(
        normed_two_all, unit_cols[:, :2].reshape(length, 2 * unit_width)
    )
    feedforward_down_term = contract_rows(cotangent_all, unit_cols[:, 2])
    feedforward_term = jnp.concatenate(
        [feedforward_in_term, feedforward_down_term], axis=1
    ).reshape(groups, shards, owned_rows, 3, unit_width)
    grad_hidden = upstream + norm_backward(grad_normed_two, normal_two, inverse_two, gain_two)
    grad_gain_two = jnp.sum(grad_normed_two * normal_two, axis=0)
    grad_shift_two = jnp.sum(grad_normed_two, axis=0)
    grad_hidden_low = grad_hidden.astype(jnp.bfloat16)
    attention_back = lax.all_gather(
        attention_weights.astype(jnp.bfloat16), ("seq", "fsdp"), axis=0, tiled=True
    )
    grad_attended = contract_cols(grad_hidden_low, attention_back[:, 3 * D :]).astype(jnp.bfloat16)
    grad_heads = lax.all_to_all(
        grad_attended.reshape(tokens, groups, local_width),
        "seq",
        split_axis=1,
        concat_axis=0,
        tiled=True,
    ).reshape(length, local_heads, HD)

    def backward_block(carry, items):
        grad_key_sum, grad_value_sum = carry
        start_row, logsum_block = items
        query_block = lax.dynamic_slice_in_dim(query_all, start_row, block_rows)
        output_block = lax.dynamic_slice_in_dim(output_heads, start_row, block_rows)
        grad_block = lax.dynamic_slice_in_dim(grad_heads, start_row, block_rows)
        scores = (
            jnp.einsum("bhd,lhd->hbl", query_block, key_all, preferred_element_type=jnp.float32)
            * score_scale
        )
        scores = jnp.where(block_mask(segment_ids, start_row, block_rows)[None], scores, neg_fill)
        probability = jnp.exp(scores - logsum_block[..., None])
        prob_low = probability.astype(jnp.bfloat16)
        grad_value_sum = grad_value_sum + jnp.einsum(
            "hbl,bhd->lhd", prob_low, grad_block, preferred_element_type=jnp.float32
        )
        grad_prob = jnp.einsum(
            "bhd,lhd->hbl", grad_block, value_all, preferred_element_type=jnp.float32
        )
        row_delta = jnp.sum(
            grad_block.astype(jnp.float32) * output_block.astype(jnp.float32), axis=-1
        )
        row_delta = jnp.transpose(row_delta)[..., None]
        grad_scores = (probability * (grad_prob - row_delta) * score_scale).astype(jnp.bfloat16)
        grad_query = jnp.einsum(
            "hbl,lhd->bhd", grad_scores, key_all, preferred_element_type=jnp.float32
        ).astype(jnp.bfloat16)
        grad_key_sum = grad_key_sum + jnp.einsum(
            "hbl,bhd->lhd", grad_scores, query_block, preferred_element_type=jnp.float32
        )
        return ((grad_key_sum, grad_value_sum), grad_query)

    zero_heads = jnp.zeros((length, local_heads, HD), jnp.float32)
    sums, grad_query_blocks = lax.scan(
        backward_block, (zero_heads, zero_heads), (block_starts, logsum_blocks)
    )
    grad_key_sum, grad_value_sum = sums
    grad_query_all = grad_query_blocks.reshape(length, local_heads, HD)
    grad_key_low = grad_key_sum.astype(jnp.bfloat16)
    grad_value_low = grad_value_sum.astype(jnp.bfloat16)
    grad_packed = jnp.stack(
        [
            grad_query_all.reshape(length, local_width),
            grad_key_low.reshape(length, local_width),
            grad_value_low.reshape(length, local_width),
        ],
        axis=1,
    )
    back_tokens = lax.all_to_all(
        grad_packed.reshape(groups, tokens, 3, local_width),
        "seq",
        split_axis=0,
        concat_axis=3,
        tiled=True,
    )[0]
    grad_query_tok = rotate(
        back_tokens[:, 0].astype(jnp.float32).reshape(tokens, H, HD), cosine, sine, half_rot, -1.0
    ).reshape(tokens, D)
    grad_key_tok = rotate(
        back_tokens[:, 1].astype(jnp.float32).reshape(tokens, H, HD), cosine, sine, half_rot, -1.0
    ).reshape(tokens, D)
    grad_projected = jnp.concatenate(
        [grad_query_tok, grad_key_tok, back_tokens[:, 2].astype(jnp.float32)], axis=1
    )
    grad_bias = jnp.sum(grad_projected, axis=0)
    grad_projected_low = grad_projected.astype(jnp.bfloat16)
    grad_normed_one = contract_cols(grad_projected_low, attention_back[:, : 3 * D])
    grad_stream = grad_hidden + norm_backward(grad_normed_one, normal_one, inverse_one, gain_one)
    grad_gain_one = jnp.sum(grad_normed_one * normal_one, axis=0)
    grad_shift_one = jnp.sum(grad_normed_one, axis=0)
    query_back = rotate(
        grad_query_all.astype(jnp.float32), cosine_all, sine_all, half_rot, -1.0
    ).astype(jnp.bfloat16)
    key_float = lax.optimization_barrier(grad_key_low).astype(jnp.float32)
    key_back = rotate(key_float, cosine_all, sine_all, half_rot, -1.0).astype(jnp.bfloat16)
    head_cols = jnp.stack(
        [
            query_back.reshape(length, local_width),
            key_back.reshape(length, local_width),
            grad_value_low.reshape(length, local_width),
        ],
        axis=1,
    )
    normed_all, grad_hidden_all = (
        lax.all_gather(normed_low, "seq", axis=0, tiled=True),
        lax.all_gather(grad_hidden_low, "seq", axis=0, tiled=True),
    )
    qkv_term = contract_rows(normed_all, head_cols.reshape(length, 3 * local_width)).reshape(
        groups, shards, owned_rows, 3, local_width
    )
    out_term = contract_rows(output_heads.reshape(length, local_width), grad_hidden_all)
    feedforward_sum, qkv_sum, out_rows = (
        lax.psum_scatter(feedforward_term, "fsdp", scatter_dimension=1, tiled=True),
        lax.psum_scatter(qkv_term, "fsdp", scatter_dimension=1, tiled=True),
        lax.psum_scatter(out_term, "fsdp", scatter_dimension=0, tiled=True),
    )
    feedforward_rows, qkv_rows = (
        lax.all_to_all(
            feedforward_sum.reshape(groups, owned_rows, 3, unit_width),
            "seq",
            split_axis=0,
            concat_axis=3,
            tiled=True,
        ),
        lax.all_to_all(
            qkv_sum.reshape(groups, owned_rows, 3, local_width),
            "seq",
            split_axis=0,
            concat_axis=3,
            tiled=True,
        ),
    )
    feedforward_grad = feedforward_rows.reshape(owned_rows, 3 * FF)
    attention_grad = jnp.concatenate([qkv_rows.reshape(owned_rows, 3 * D), out_rows], axis=1)
    vector_term = jnp.stack(
        [
            grad_gain_one,
            grad_shift_one,
            grad_bias[:D],
            grad_bias[D : 2 * D],
            grad_bias[2 * D :],
            grad_gain_two,
            grad_shift_two,
        ]
    )
    vector_grad = lax.psum_scatter(vector_term, ("seq", "fsdp"), scatter_dimension=1, tiled=True)
    attention_new, attention_state = adamw_update(
        attention_weights, attention_grad, attention_moments, decay_rate
    )
    feedforward_new, feedforward_state = adamw_update(
        feedforward_weights, feedforward_grad, feedforward_moments, decay_rate
    )
    vector_new, vector_state = adamw_update(norm_vectors, vector_grad, vector_moments, 0.0)
    return (
        result[None],
        grad_stream[None],
        attention_grad,
        feedforward_grad,
        vector_grad,
        attention_new,
        feedforward_new,
        vector_new,
        attention_state,
        feedforward_state,
        vector_state,
    )


def solution(mesh):
    in_specs = (
        P("fsdp", "seq", None),
        P("fsdp", None),
        P(("seq", "fsdp"), None),
        P(("seq", "fsdp"), None),
        P(None, ("seq", "fsdp")),
        P(None, ("seq", "fsdp"), None),
        P(None, ("seq", "fsdp"), None),
        P(None, None, ("seq", "fsdp")),
        P("fsdp", "seq", None),
    )
    out_specs = (
        P("fsdp", "seq", None),
        P("fsdp", "seq", None),
        P(("seq", "fsdp"), None),
        P(("seq", "fsdp"), None),
        P(None, ("seq", "fsdp")),
        P(("seq", "fsdp"), None),
        P(("seq", "fsdp"), None),
        P(None, ("seq", "fsdp")),
        P(None, ("seq", "fsdp"), None),
        P(None, ("seq", "fsdp"), None),
        P(None, None, ("seq", "fsdp")),
    )
    return jax.shard_map(body, mesh=mesh, in_specs=in_specs, out_specs=out_specs, check_vma=False)
```

profile of v0, /device:TPU:0, one launch (start us, length us, event | category | flops | bytes accessed | tf_op | source)
XLA Modules:
  0.0 1546.8 jit_solution(579095398711331693)
XLA Ops:
  10.0 3.9 convert_element_type.158
  13.9 73.3 %all-gather = bf16[32,64,7]{1,2,0:T(8,128)(2,1)S(1)} all-gather(bf16[1,64,7]{1,2,0:T(8,128)(2,1)S(1)} %convert_bitcast_fusion), channel_id=1, replica_groups=mesh['seq'=8,'fsdp'=4] {'seq','fsdp'}, dimensions={0}, use_global_device_ids=true | all-gather | bytes 29568 | tf_op jit(solution)/shard_map/all_gather | solution.py:127
  90.8 118.3 %all-gather.8.cloned.1.call-done = bf16[2048,8192]{1,0:T(8,128)(2,1)} async-done(((bf16[64,8192]{1,0:T(8,128)(2,1)}), bf16[2048,8192]{1,0:T(8,128)(2,1)}) %all-gather.8.cloned.1.call-update) | async-done | bytes 33554448 | tf_op jit(solution)/shard_map/all_gather | solution.py:126
  209.1 10.0 fusion.53
  237.4 20.2 %all-to-all-done = bf16[128,3,8,256]{0,3,1,2:T(8,128)(2,1)S(1)} async-done(((bf16[128,3,8,256]{0,3,1,2:T(8,128)(2,1)}), bf16[128,3,8,256]{0,3,1,2:T(8,128)(2,1)S(1)}, u32[]{:S(2)}, u32[]{:S(2)}) %all-to-all-start) | async-done | bytes 1572896 | tf_op jit(solution)/shard_map/all_to_all | solution.py:162
  262.0 22.3 %while.27 = (s32[]{:T(128)}, bf16[2,512,4,64]{1,3,2,0:T(8,128)(2,1)S(1)}, f32[2,4,512]{2,1,0:T(4,128)S(1)}, s32[2]{0:T(128)S(1)}, s32[1,1024]{1,0:T(1,128)S(1)},...) while((s32[]{:T(128)}, ...), condition=%wide.region_7.8_spmd, body=%wide.region_4.7_spmd.sunk | while | flops 563739136 | bytes 31013084 | solution.py:183
  288.0 4.4 all-to-all-start.1
  294.5 13.6 all-to-all-done.1
  308.1 4.9 fusion.114
  313.6 268.4 %all-gather.10.cloned.1.call-done = bf16[2048,16896]{1,0:T(8,128)(2,1)} async-done(((bf16[64,16896]{1,0:T(8,128)(2,1)}), bf16[2048,16896]{1,0:T(8,128)(2,1)}) %all-gather.10.cloned.1.call-update) | async-done | bytes 69206032 | tf_op jit(solution)/shard_map/all_gather | solution.py:129
  582.0 19.2 %fusion.39 = f32[128,11264]{1,0:T(8,128)} fusion(bf16[128,2048]{1,0:T(8,128)(2,1)S(1)} %add_convert_fusion, bf16[2048,16896]{1,0:T(8,128)(2,1)} %all-gather.10.cloned.1.call-done), kind=kOutput, calls=%fused_computation.48 | convolution fusion | flops 5905580032 | bytes 52428800 | tf_op jit(solution)/shard_map/dot_general | solution.py:197
  601.2 14.2 multiply_convert_fusion.2
  615.4 23.5 %multiply_reduce_fusion.1 = (f32[2048]{0:T(1024)}, f32[128]{0:T(128)S(1)}, f32[128]{0:T(128)S(1)}, f32[2048]{0:T(1024)}, f32[128,2048]{1,0:T(8,128)}) fusion(f32[128,2048]{1,0:T(8,128)S(1)} %get-tuple-element.375, f32[128]{0:T(128)S(1)} %add_rsqrt_fusion, f32[128]{0:T(128)S(1)} %broadcast_multiply_fusion.6, f32[2048]{0:T(1024)S(1)} %bitcast.374, ...), kind=kOutput, calls=%fused_computation.129 | convolution fusion | flops 5913702400 | bytes 51144704 | tf_op jit(solution)/shard_map/dot_general | solution.py:79
  641.9 6.5 fusion.76
  649.2 4.1 all-to-all-start.2
  653.5 6.5 copy.175
  667.3 46.8 %while.28 = (s32[]{:T(128)}, f32[1024,4,64]{0,2,1:T(8,128)S(1)}, f32[1024,4,64]{0,2,1:T(8,128)}, bf16[2,512,4,64]{1,3,2,0:T(8,128)(2,1)}, s32[2]{0:T(128)S(1)}, ...) while((s32[]{:T(128)}, f32[1024,4,64]{0,2,1:T(8,128)S(1)}, ...), condition=%wide.region_14.15_spmd.clone, body=%wide.region_12.14_spmd.clone.sunk | while | flops 1368521216 | bytes 149748272 | solution.py:286
  673.0 6.5 multiply_convert_fusion.5
  685.1 3.7 fusion.176
  696.8 6.6 multiply_convert_fusion.5
  708.2 3.7 fusion.176
  716.9 5.3 fusion.90
  740.6 9.7 all-to-all-done.3
  750.3 4.6 all-to-all-start.5
  757.9 14.7 multiply_reduce_fusion.2
  774.4 31.0 %all-to-all-done.5 = bf16[128,3,8,704]{0,3,1,2:T(8,128)(2,1)} async-done(((bf16[128,3,8,704]{0,3,1,2:T(8,128)(2,1)}), bf16[128,3,8,704]{0,3,1,2:T(8,128)(2,1)}, u32[]{:S(2)}, u32[]{:S(2)}) %all-to-all-start.5) | async-done | bytes 4325408 | tf_op jit(solution)/shard_map/all_to_all | solution.py:225
  805.4 7.2 copy.183
  812.6 7.7 squeeze.57
  820.3 3.7 slice.281
  824.0 8.2 convolution_bitcast_fusion.1
  832.2 9.0 fusion.116
  841.2 6.4 pad_maximum_fusion
  847.6 33.1 %reshape.553 = f32[8,4,64,3,704]{2,1,0,4,3:T(4,128)} reshape(f32[2048,2112]{0,1:T(8,128)} %pad_maximum_fusion) | data formatting | bytes 34603008 | tf_op jit(solution)/shard_map/reshape | solution.py:236
  880.8 34.2 %copy.185 = f32[8,4,64,3,704]{4,2,3,0,1:T(8,128)} copy(f32[8,4,64,3,704]{2,1,0,4,3:T(4,128)} %reshape.553) | data formatting | bytes 34603008 | tf_op jit(solution)/shard_map/reshape | solution.py:236
  916.4 26.9 %all-reduce.3.cloned.1.call-done = f32[8,4,64,3,256]{4,2,3,1,0:T(8,128)} async-done(((f32[8,4,64,3,256]{4,2,3,1,0:T(8,128)}), f32[8,4,64,3,256]{4,2,3,1,0:T(8,128)}) %all-reduce.3.cloned.1.call-update) | async-done | bytes 6291472
  946.6 4.3 all-to-all-start.4
  951.2 41.1 %all-gather.14.cloned.1.call-done = bf16[1024,2048]{1,0:T(8,128)(2,1)} async-done(((bf16[128,2048]{1,0:T(8,128)(2,1)}), bf16[1024,2048]{1,0:T(8,128)(2,1)}) %all-gather.14.cloned.1.call-update) | async-done | bytes 4194320 | tf_op jit(solution)/shard_map/all_gather | solution.py:338
  992.2 4.8 fusion.115
  997.1 13.1 fusion.70
  1011.7 120.2 %reduce-scatter.13.cloned.1.call-done = f32[64,7]{1,0:T(8,128)} async-done(((f32[2048,7]{1,0:T(8,128)}), f32[64,7]{1,0:T(8,128)}) %reduce-scatter.13.cloned.1.call-update) | async-done | bytes 1808
  1140.6 304.0 %reduce-scatter.11.cloned.1.call-done = f32[8,1,64,3,704]{4,2,3,0,1:T(8,128)} async-done(((f32[8,4,64,3,704]{4,2,3,0,1:T(8,128)}), f32[8,1,64,3,704]{4,2,3,0,1:T(8,128)}) %reduce-scatter.11.cloned.1.call-update) | async-done | bytes 4325392 | tf_op jit(solution)/shard_map/reduce_scatter | solution.py:345
  1444.6 4.6 all-to-all-start.6
  1449.2 42.7 %reduce-scatter.9.cloned.1.call-done = f32[64,2048]{1,0:T(8,128)} async-done(((f32[256,2048]{1,0:T(8,128)}), f32[64,2048]{1,0:T(8,128)}) %reduce-scatter.9.cloned.1.call-update) | async-done | bytes 524304 | tf_op jit(solution)/shard_map/reduce_scatter | solution.py:347
  1503.9 7.3 copy.186
  1511.2 5.8 reshape.543
  1517.0 5.8 reshape.544
  1522.8 9.1 multiply_subtract_fusion
  1535.4 4.1 pad_maximum_fusion.1
  (322 shorter events, 143.0 us)
Async XLA Ops:
  7.2 201.9 %all-gather.8.cloned.1.call-start = ((), (), s32[]{:S(2)}) async-start(), calls=%async_computation.10 | async-start | bytes 34603008 | tf_op jit(solution)/shard_map/all_gather | solution.py:126
  9.9 77.4 %copy-start.31 = (s32[1,1024]{1,0:T(1,128)S(1)}, s32[1,1024]{1,0:T(1,128)}, u32[]{:S(2)}) copy-start(s32[1,1024]{1,0:T(1,128)} %param.14) | copy-start | bytes 12292
  9.9 77.9 %copy-start.3 = (f32[1,128,2048]{2,1,0:T(8,128)S(1)}, f32[1,128,2048]{2,1,0:T(8,128)}, u32[]{:S(2)}) copy-start(f32[1,128,2048]{2,1,0:T(8,128)} %param.13) | copy-start | bytes 3145732
  10.0 572.1 %all-gather.10.cloned.1.call-start = ((), (), s32[]{:S(2)}) async-start(), calls=%async_computation.11 | async-start | bytes 71368704 | tf_op jit(solution)/shard_map/all_gather | solution.py:129
  89.6 140.6 %copy-start.43 = (f32[128,8]{0,1:T(8,128)}, f32[128,8]{0,1:T(8,128)S(1)}, u32[]{:S(2)}) copy-start(f32[128,8]{0,1:T(8,128)S(1)} %get-tuple-element.378) | copy-start | bytes 12292
  90.3 128.8 %copy-start.41 = (f32[1,2048]{1,0:T(1,128)}, f32[1,2048]{1,0:T(1,128)S(1)}, u32[]{:S(2)}) copy-start(f32[1,2048]{1,0:T(1,128)S(1)} %get-tuple-element.358) | copy-start | bytes 24580
  90.3 128.8 %copy-start.54 = (f32[128]{0:T(128)}, f32[128]{0:T(128)S(1)}, u32[]{:S(2)}) copy-start(f32[128]{0:T(128)S(1)} %broadcast_multiply_fusion.7) | copy-start | bytes 1540
  90.5 128.6 %copy-start.56 = (f32[128]{0:T(128)}, f32[128]{0:T(128)S(1)}, u32[]{:S(2)}) copy-start(f32[128]{0:T(128)S(1)} %add_rsqrt_fusion.1) | copy-start | bytes 1540
  90.8 118.3 %copy-start.30 = (bf16[128,2048]{1,0:T(8,128)(2,1)}, bf16[128,2048]{1,0:T(8,128)(2,1)S(1)}, u32[]{:S(2)}) copy-start(bf16[128,2048]{1,0:T(8,128)(2,1)S(1)} %add_convert_fusion.1) | copy-start | bytes 1572868
  221.1 9.1 copy-start.47
  233.0 24.5 %all-to-all-start = ((bf16[128,3,8,256]{0,3,1,2:T(8,128)(2,1)}), bf16[128,3,8,256]{0,3,1,2:T(8,128)(2,1)S(1)}, u32[]{:S(2)}, u32[]{:S(2)}) async-start(bf16[128,3,8,256]{0,3,1,2:T(8,128)(2,1)} %copy.162), calls=%async_computation | async-start | bytes 3145728 | tf_op jit(solution)/shard_map/all_to_all | solution.py:162
  236.6 416.9 %all-gather.12.cloned.1.call-start = ((), (), s32[]{:S(2)}) async-start(), calls=%async_computation.12 | async-start | bytes 4718592 | tf_op jit(solution)/shard_map/all_gather | solution.py:337
  284.4 23.7 %copy-start.19 = (bf16[2,512,4,64]{1,3,2,0:T(8,128)(2,1)}, bf16[2,512,4,64]{1,3,2,0:T(8,128)(2,1)S(1)}, u32[]{:S(2)}) copy-start(bf16[2,512,4,64]{1,3,2,0:T(8,128)(2,1)S(1)} %get-tuple-element.128) | copy-start | bytes 1572868
  284.9 23.2 %copy-start.14 = (bf16[2,512,4,64]{1,0,3,2:T(2,128)(2,1)}, bf16[2,512,4,64]{1,0,3,2:T(2,128)(2,1)S(1)}, u32[]{:S(2)}) copy-start(bf16[2,512,4,64]{1,0,3,2:T(2,128)(2,1)S(1)} %copy.167) | copy-start | bytes 1572868
  288.0 20.1 %all-to-all-start.1 = ((bf16[8,128,256]{1,2,0:T(8,128)(2,1)}), bf16[8,128,256]{1,2,0:T(8,128)(2,1)}, u32[]{:S(2)}, u32[]{:S(2)}) async-start(bf16[8,128,256]{1,2,0:T(8,128)(2,1)} %copy.168), calls=%async_computation.1 | async-start | bytes 1048576 | tf_op jit(solution)/shard_map/all_to_all | solution.py:185
  292.3 531.6 %all-gather.18.cloned.1.call-start = ((), (), s32[]{:S(2)}) async-start(), calls=%async_computation.16 | async-start | bytes 4718592 | tf_op jit(solution)/shard_map/all_gather | solution.py:228
  308.1 5.2 copy-start.45
  313.0 325.9 %copy-start.7 = (f32[128,2048]{1,0:T(8,128)}, f32[128,2048]{1,0:T(8,128)S(1)}, u32[]{:S(2)}) copy-start(f32[128,2048]{1,0:T(8,128)S(1)} %get-tuple-element.375) | copy-start | bytes 3145732
  313.6 287.6 %copy-start.29 = (bf16[128,2048]{1,0:T(8,128)(2,1)}, bf16[128,2048]{1,0:T(8,128)(2,1)S(1)}, u32[]{:S(2)}) copy-start(bf16[128,2048]{1,0:T(8,128)(2,1)S(1)} %add_convert_fusion) | copy-start | bytes 1572868
  313.6 287.6 %copy-start.27 = (bf16[128,2048]{1,0:T(8,128)(2,1)S(1)}, bf16[128,2048]{1,0:T(8,128)(2,1)}, u32[]{:S(2)}) copy-start(bf16[128,2048]{1,0:T(8,128)(2,1)} %bitcast_convert_fusion) | copy-start | bytes 1572868
  615.4 23.5 %copy-start.24 = (f32[1,128,2048]{2,1,0:T(8,128)S(1)}, f32[1,128,2048]{2,1,0:T(8,128)}, u32[]{:S(2)}) copy-start(f32[1,128,2048]{2,1,0:T(8,128)} %param.21) | copy-start | bytes 3145732
  649.2 13.9 all-to-all-start.2
  653.4 178.8 %all-gather.16.cloned.1.call-start = ((), (), s32[]{:S(2)}) async-start(), calls=%async_computation.15 | async-start | bytes 4718592 | tf_op jit(solution)/shard_map/all_gather | solution.py:227
  653.5 6.5 copy-start.20
  660.1 283.2 %all-reduce.3.cloned.1.call-start = ((), (), s32[]{:S(2)}) async-start(), calls=%async_computation.19 | async-start | bytes 12582912
  671.4 8.2 copy-start.1
  679.6 5.3 copy-start.2
  679.6 5.6 copy-start.32
  695.1 8.2 copy-start.1
  722.2 270.0 %all-gather.14.cloned.1.call-start = ((), (), s32[]{:S(2)}) async-start(), calls=%async_computation.13 | async-start | bytes 4718592 | tf_op jit(solution)/shard_map/all_gather | solution.py:338
  725.8 24.5 %all-to-all-start.3 = ((bf16[8,128,3,256]{1,3,2,0:T(8,128)(2,1)}), bf16[8,128,3,256]{1,3,2,0:T(8,128)(2,1)S(1)}, u32[]{:S(2)}, u32[]{:S(2)}) async-start(bf16[8,128,3,256]{1,3,2,0:T(8,128)(2,1)} %copy.173), calls=%async_computation.3 | async-start | bytes 3145728 | tf_op jit(solution)/shard_map/all_to_all | solution.py:301
  750.3 55.1 %all-to-all-start.5 = ((bf16[128,3,8,704]{0,3,1,2:T(8,128)(2,1)}), bf16[128,3,8,704]{0,3,1,2:T(8,128)(2,1)}, u32[]{:S(2)}, u32[]{:S(2)}) async-start(bf16[128,3,8,704]{0,3,1,2:T(8,128)(2,1)} %copy.182), calls=%async_computation.6 | async-start | bytes 8650752 | tf_op jit(solution)/shard_map/all_to_all | solution.py:225
  754.9 377.1 %reduce-scatter.13.cloned.1.call-start = ((), (), s32[]{:S(2)}) async-start(), calls=%async_computation.18 | async-start | bytes 1081344
  757.9 14.7 copy-start.51
  757.9 14.7 copy-start.52
  774.1 670.5 %reduce-scatter.11.cloned.1.call-start = ((), (), s32[]{:S(2)}) async-start(), calls=%async_computation.17 | async-start | bytes 23592960 | tf_op jit(solution)/shard_map/reduce_scatter | solution.py:345
  832.2 9.0 copy-start.13
  946.6 187.4 %all-to-all-start.4 = ((f32[8,64,3,256]{3,1,2,0:T(8,128)}), f32[8,64,3,256]{3,1,2,0:T(8,128)}, u32[]{:S(2)}, u32[]{:S(2)}) async-start(f32[8,64,3,256]{3,1,2,0:T(8,128)} %dynamic-slice_bitcast_fusion.1), calls=%async_computation.4 | async-start | bytes 3145728 | tf_op jit(solution)/shard_map/all_to_all | solution.py:357
  950.9 541.0 %reduce-scatter.9.cloned.1.call-start = ((), (), s32[]{:S(2)}) async-start(), calls=%async_computation.14 | async-start | bytes 2621440 | tf_op jit(solution)/shard_map/reduce_scatter | solution.py:347
  997.1 13.2 copy-start.25
  997.1 13.2 copy-start.35
  1010.3 122.5 %copy-start.50 = (f32[7,64]{1,0:T(8,128)S(1)}, f32[7,64]{1,0:T(8,128)}, u32[]{:S(2)}) copy-start(f32[7,64]{1,0:T(8,128)} %param.17) | copy-start | bytes 5380
  1132.8 6.3 copy-start.48
  1444.6 59.3 %all-to-all-start.6 = ((f32[8,64,3,704]{3,1,2,0:T(8,128)}), f32[8,64,3,704]{3,1,2,0:T(8,128)}, u32[]{:S(2)}, u32[]{:S(2)}) async-start(f32[8,64,3,704]{3,1,2,0:T(8,128)} %bitcast.333), calls=%async_computation.8 | async-start | bytes 9437184 | tf_op jit(solution)/shard_map/all_to_all | solution.py:350
  1517.0 15.0 slice-start
  1522.8 9.1 slice-start.1
  1522.8 10.0 slice-start.2
  1522.8 11.3 copy-start.5
  (42 other events, 104.2 us)
Sparse Core Ops, SparseCore 0:
  11.5 197.5 all-gather.7
  212.5 369.5 all-gather.9
  583.9 34.7 all-gather.11
  620.4 36.5 all-gather.17
  660.2 36.9 all-gather.15
  722.4 220.8 all-reduce.2
  945.1 47.0 all-gather.13
  994.5 137.4 reduce-scatter.12
  1134.3 310.2 reduce-scatter.10
  1447.3 44.5 reduce-scatter.8
where the time goes:
time: 1560 us; the launch traced here: 1550 us
  waiting for transfers between devices  1000 us (64%)
  local copies, waits for them, and re-layouts  180 us (12%)
  matrix products  176 us (11%)
  blocking collectives  73.3 us (5%)
  other arithmetic  62.2 us (4%)
  starting transfers between devices  30.6 us (2%)
  between operations  15.6 us (1%)
    reduce_scatter x1, waiting for transfers between devices, body(): lax.psum_scatter(feedforward_term, 'fsdp', scatter_dimension=1, tiled=True)  304 us
    all_gather x1, waiting for transfers between devices, body(): lax.all_gather(feedforward_weights.astype(jnp.bfloat16), ('seq', 'fsdp'),...  268 us
    unnamed x12, waiting for transfers between devices  148 us
    all_gather x1, waiting for transfers between devices, body(): lax.all_gather(attention_weights.astype(jnp.bfloat16), ('seq', 'fsdp'), a...  118 us
    all_gather x1, blocking collectives, body(): lax.all_gather(norm_vectors.astype(jnp.bfloat16), ('seq', 'fsdp'), axis=1...  73.3 us
    reshape x2, local copies, waits for them, and re-layouts, body(): feedforward_term = jnp.concatenate([feedforward_in_term, feedforward_down...  67.4 us
    dot_general x4, matrix products, contract_cols(): lax.dot_general(left, right, (((1,), (1,)), ((), ())), preferred_element_...  57.9 us
    reduce_scatter x1, waiting for transfers between devices, body(): lax.psum_scatter(out_term, 'fsdp', scatter_dimension=0, tiled=True)  42.7 us
  transfers between devices with their start and end apart: 17, of which 13 were waited for; matrix products, arithmetic and copies ran while one was open for 24% of the time, Pallas kernels for 0%

commit v1 on v0

v1 whole, which is shorter than its diff:
```python
import functools

import jax
import jax.numpy as jnp
from jax import lax
from jax.experimental import pallas as pl
from jax.experimental.pallas import tpu as pltpu
from jax.sharding import PartitionSpec as P

D = 2048
H = 32
HD = 64
ROT = 16
FF = 5632

norm_epsilon = 1e-05
rope_base = 10000.0
neg_fill = -1e30
learn_rate = 0.01
beta_first = 0.9
beta_second = 0.95
adam_epsilon = 1e-08
decay_rate = 0.1
adam_step = 2.0

MESH_IDS = pl.DeviceIdType.MESH
bf16 = jnp.bfloat16
f32 = jnp.float32


def document_positions(segment_ids):
    length = segment_ids.shape[0]
    indices = jnp.arange(length, dtype=jnp.int32)
    changes = jnp.concatenate(
        [jnp.ones((1,), dtype=jnp.bool_), segment_ids[1:] != segment_ids[:-1]]
    )
    starts = lax.cummax(jnp.where(changes, indices, jnp.zeros_like(indices)), axis=0)
    return indices - starts


def rotary_tables(positions, half_rot):
    powers = jnp.arange(half_rot, dtype=jnp.float32) / float(half_rot)
    inverse = rope_base ** (-powers)
    angles = positions.astype(jnp.float32)[:, None] * inverse[None, :]
    return (jnp.cos(angles), jnp.sin(angles))


def rotate(values, cosine, sine, half_rot, direction):
    first = values[..., :half_rot]
    second = values[..., half_rot : 2 * half_rot]
    cosine_wide = cosine[:, None, :]
    sine_wide = sine[:, None, :] * direction
    return jnp.concatenate(
        [
            first * cosine_wide - second * sine_wide,
            second * cosine_wide + first * sine_wide,
            values[..., 2 * half_rot :],
        ],
        axis=-1,
    )


def norm_forward(values, gain, shift):
    centred = values - jnp.mean(values, axis=-1, keepdims=True)
    inverse = lax.rsqrt(jnp.mean(centred * centred, axis=-1, keepdims=True) + norm_epsilon)
    normal_part = centred * inverse
    return (normal_part * gain + shift, normal_part, inverse)


def norm_backward(upstream, normal_part, inverse, gain):
    scaled = upstream * gain
    return inverse * (
        scaled
        - jnp.mean(scaled, axis=-1, keepdims=True)
        - normal_part * jnp.mean(scaled * normal_part, axis=-1, keepdims=True)
    )


def contract_rows(left, right, out=jnp.float32):
    return lax.dot_general(left, right, (((0,), (0,)), ((), ())), preferred_element_type=out)


def contract_cols(left, right, out=jnp.float32):
    return lax.dot_general(left, right, (((1,), (1,)), ((), ())), preferred_element_type=out)


def block_mask(segment_ids, start_row, block_rows):
    total_keys = segment_ids.shape[0]
    row_ids = start_row + jnp.arange(block_rows, dtype=jnp.int32)
    col_ids = jnp.arange(total_keys, dtype=jnp.int32)
    row_segments = lax.dynamic_slice_in_dim(segment_ids, start_row, block_rows)
    return (col_ids[None, :] <= row_ids[:, None]) & (segment_ids[None, :] == row_segments[:, None])


def adamw_update(weight, grad, moments, decay):
    first = beta_first * moments[0] + (1.0 - beta_first) * grad
    second = beta_second * moments[1] + (1.0 - beta_second) * grad * grad
    correct_one = 1.0 - beta_first**adam_step
    correct_two = 1.0 - beta_second**adam_step
    update = first / correct_one / (jnp.sqrt(second / correct_two) + adam_epsilon)
    return (weight - learn_rate * (update + decay * weight), jnp.stack([first, second]))


def plane_places():
    me = lax.axis_index("seq")
    core = me % 2
    first = 2 + 2 * core
    second = 4 - 2 * core
    bit_first = (me // first) % 2
    bit_second = (me // second) % 2
    sibling = me + 1 - 2 * core
    near = me + first * (1 - 2 * bit_first)
    far = me + second * (1 - 2 * bit_second)
    corner = near + second * (1 - 2 * bit_second)
    return me, sibling, near, far, corner


def greet(others):
    barrier = pltpu.get_barrier_semaphore()
    for other in others:
        pl.semaphore_signal(barrier, inc=1, device_id={"seq": other}, device_id_type=MESH_IDS)
    pl.semaphore_wait(barrier, len(others))


def gather_kernel(x_ref, o_ref, local_sem, send_sem, recv_sem):
    me, sibling, near, far, corner = plane_places()

    def copy(source, slot, index, target):
        return pltpu.make_async_remote_copy(
            src_ref=source,
            dst_ref=o_ref.at[slot],
            send_sem=send_sem.at[index],
            recv_sem=recv_sem.at[index],
            device_id={"seq": target},
            device_id_type=MESH_IDS,
        )

    greet((sibling, near, far))
    own = pltpu.make_async_copy(x_ref, o_ref.at[me], local_sem)
    own.start()
    to_near = copy(x_ref, me, 0, near)
    to_far = copy(x_ref, me, 1, far)
    to_sibling = copy(x_ref, me, 2, sibling)
    to_near.start()
    to_far.start()
    to_sibling.start()
    to_near.wait_recv()
    near_far = copy(o_ref.at[near], near, 3, far)
    near_far.start()
    near_sibling = copy(o_ref.at[near], near, 4, sibling)
    near_sibling.start()
    to_far.wait_recv()
    far_sibling = copy(o_ref.at[far], far, 5, sibling)
    far_sibling.start()
    near_far.wait_recv()
    corner_sibling = copy(o_ref.at[corner], corner, 6, sibling)
    corner_sibling.start()
    for one in (to_sibling, near_sibling, far_sibling, corner_sibling):
        one.wait_recv()
    for one in (to_near, to_far, to_sibling, near_far, near_sibling, far_sibling, corner_sibling):
        one.wait_send()
    own.wait()


def plane_gather(values, collective_id):
    rows, cols = values.shape
    out = pl.pallas_call(
        gather_kernel,
        out_shape=jax.ShapeDtypeStruct((8, rows, cols), values.dtype),
        in_specs=[pl.BlockSpec(memory_space=pltpu.VMEM)],
        out_specs=pl.BlockSpec(memory_space=pl.ANY),
        scratch_shapes=[
            pltpu.SemaphoreType.DMA,
            pltpu.SemaphoreType.DMA((7,)),
            pltpu.SemaphoreType.DMA((7,)),
        ],
        compiler_params=pltpu.CompilerParams(collective_id=collective_id, has_side_effects=True),
        name="plane_gather",
    )(values)
    return out.reshape(8 * rows, cols)


def scatter_kernel(p_ref, o_ref, mine, pair, near_out, near_in, far_out, far_in, local_sem, send_sem, recv_sem):
    me, sibling, near, far, corner = plane_places()
    flip = sibling - me
    order = (corner, near, far, me)
    sibling_order = (corner, far, near, me)

    def copy(source, target_ref, index, target):
        return pltpu.make_async_remote_copy(
            src_ref=source,
            dst_ref=target_ref,
            send_sem=send_sem.at[index],
            recv_sem=recv_sem.at[index],
            device_id={"seq": target},
            device_id_type=MESH_IDS,
        )

    greet((sibling, near, far))
    pairs = []
    locals_ = []
    for index, block in enumerate(order):
        one = copy(p_ref.at[sibling_order[index] + flip], pair.at[index], index, sibling)
        one.start()
        pairs.append(one)
        own = pltpu.make_async_copy(p_ref.at[block], mine.at[index], local_sem.at[index])
        own.start()
        locals_.append(own)
    for index in range(2):
        pairs[index].wait_recv()
        locals_[index].wait()
        near_out[index] = (mine[index].astype(f32) + pair[index].astype(f32)).astype(near_out.dtype)
        step = copy(near_out.at[index], near_in.at[index], 4 + index, near)
        step.start()
        pairs.append(step)
    for index in range(2, 4):
        pairs[index].wait_recv()
        locals_[index].wait()
    pairs[4].wait_recv()
    far_out[...] = (
        mine[2].astype(f32) + pair[2].astype(f32) + near_in[0].astype(f32)
    ).astype(far_out.dtype)
    last = copy(far_out, far_in, 6, far)
    last.start()
    pairs[5].wait_recv()
    o_ref[...] = mine[3].astype(f32) + pair[3].astype(f32) + near_in[1].astype(f32)
    last.wait_recv()
    o_ref[...] += far_in[...].astype(f32)
    for one in pairs:
        one.wait_send()
    last.wait_send()


def plane_scatter(values, collective_id):
    rows, cols = values.shape
    rows = rows // 8
    return pl.pallas_call(
        scatter_kernel,
        out_shape=jax.ShapeDtypeStruct((rows, cols), f32),
        in_specs=[pl.BlockSpec(memory_space=pl.ANY)],
        out_specs=pl.BlockSpec(memory_space=pltpu.VMEM),
        scratch_shapes=[
            pltpu.VMEM((4, rows, cols), values.dtype),
            pltpu.VMEM((4, rows, cols), values.dtype),
            pltpu.VMEM((2, rows, cols), values.dtype),
            pltpu.VMEM((2, rows, cols), values.dtype),
            pltpu.VMEM((rows, cols), values.dtype),
            pltpu.VMEM((rows, cols), values.dtype),
            pltpu.SemaphoreType.DMA((4,)),
            pltpu.SemaphoreType.DMA((7,)),
            pltpu.SemaphoreType.DMA((7,)),
        ],
        compiler_params=pltpu.CompilerParams(
            collective_id=collective_id, has_side_effects=True, vmem_limit_bytes=32 << 20
        ),
        name="plane_scatter",
    )(values.reshape(8, rows, cols))


def gather_tokens(values, collective_id):
    if lax.axis_size("seq") == 8:
        return plane_gather(values, collective_id)
    return lax.all_gather(values, "seq", axis=0, tiled=True)


def scatter_tokens(values, collective_id):
    if lax.axis_size("seq") == 8:
        return plane_scatter(values.astype(bf16), collective_id)
    return lax.psum_scatter(values, "seq", scatter_dimension=0, tiled=True)


def body(
    stream,
    segments,
    attention_weights,
    feedforward_weights,
    norm_vectors,
    attention_moments,
    feedforward_moments,
    vector_moments,
    cotangent,
):
    groups = lax.axis_size("seq")
    shards = lax.axis_size("fsdp")
    my_rank = lax.axis_index("seq")
    tokens = stream.shape[1]
    length = tokens * groups
    local_heads = H // groups
    local_width = local_heads * HD
    unit_width = FF // groups
    owned_rows = D // (groups * shards)
    plane_rows = groups * owned_rows
    half_rot = ROT // 2
    score_scale = float(HD) ** (-0.5)
    block_rows = min(512, length)
    block_starts = jnp.arange(length // block_rows, dtype=jnp.int32) * block_rows

    def to_order(values):
        lead = values.shape[:-1]
        return values.reshape(*lead, groups, shards, owned_rows).swapaxes(-3, -2).reshape(*lead, D)

    def from_order(values):
        lead = values.shape[:-1]
        return values.reshape(*lead, shards, groups, owned_rows).swapaxes(-3, -2).reshape(*lead, D)

    def spread_columns(values, parts, width):
        blocks = values.reshape(owned_rows, parts, groups, width).transpose(2, 0, 1, 3)
        blocks = blocks.reshape(groups, owned_rows, parts * width)
        moved = lax.all_to_all(blocks, "seq", split_axis=0, concat_axis=0, tiled=True)
        return moved.reshape(plane_rows, parts * width)

    attention_low = attention_weights.astype(bf16)
    feedforward_low = feedforward_weights.astype(bf16)
    vector_low = lax.all_gather(norm_vectors.astype(bf16), ("seq", "fsdp"), axis=1, tiled=True)
    qkv_weights = lax.all_gather(
        spread_columns(attention_low[:, : 3 * D], 3, local_width), "fsdp", axis=0, tiled=True
    )
    out_weights = lax.all_gather(to_order(attention_low[:, 3 * D :]), "fsdp", axis=0, tiled=True)
    in_weights = lax.all_gather(
        spread_columns(feedforward_low[:, : 2 * FF], 2, unit_width), "fsdp", axis=0, tiled=True
    )
    down_weights = lax.all_gather(
        spread_columns(feedforward_low[:, 2 * FF :], 1, unit_width), "fsdp", axis=0, tiled=True
    )

    vector_full = vector_low.astype(f32)
    ordered = to_order(vector_full)
    gain_one, shift_one, gain_two, shift_two = [ordered[i] for i in (0, 1, 5, 6)]
    bias = lax.dynamic_slice_in_dim(
        vector_full[2:5], my_rank * local_width, local_width, axis=1
    ).reshape(3 * local_width)
    segment_ids = segments[0]
    cosine, sine = rotary_tables(document_positions(segment_ids), half_rot)

    inputs = to_order(stream[0])
    upstream = to_order(cotangent[0])
    normed_one, normal_one, inverse_one = norm_forward(inputs, gain_one, shift_one)
    normed_all = gather_tokens(normed_one.astype(bf16), 1)
    cotangent_all = gather_tokens(upstream.astype(bf16), 2)
    projected = (
        jnp.dot(normed_all, qkv_weights, preferred_element_type=f32) + bias
    ).reshape(length, 3, local_heads, HD)
    query_all = rotate(projected[:, 0], cosine, sine, half_rot, 1.0).astype(bf16)
    key_all = rotate(projected[:, 1], cosine, sine, half_rot, 1.0).astype(bf16)
    value_all = projected[:, 2].astype(bf16)

    def forward_block(start_row):
        query_block = lax.dynamic_slice_in_dim(query_all, start_row, block_rows)
        scores = (
            jnp.einsum("bhd,lhd->hbl", query_block, key_all, preferred_element_type=jnp.float32)
            * score_scale
        )
        scores = jnp.where(block_mask(segment_ids, start_row, block_rows)[None], scores, neg_fill)
        row_max = jnp.max(scores, axis=-1, keepdims=True)
        weights_raw = jnp.exp(scores - row_max)
        row_sum = jnp.sum(weights_raw, axis=-1, keepdims=True)
        probability = (weights_raw / row_sum).astype(jnp.bfloat16)
        output_block = jnp.einsum(
            "hbl,lhd->bhd", probability, value_all, preferred_element_type=jnp.float32
        ).astype(jnp.bfloat16)
        return (output_block, (row_max + jnp.log(row_sum))[..., 0])

    output_blocks, logsum_blocks = lax.map(forward_block, block_starts)
    output_heads = output_blocks.reshape(length, local_heads, HD)
    attended = output_heads.reshape(length, local_width)
    hidden = inputs + scatter_tokens(jnp.dot(attended, out_weights, preferred_element_type=f32), 3)
    normed_two, normal_two, inverse_two = norm_forward(hidden, gain_two, shift_two)
    normed_two_all = gather_tokens(normed_two.astype(bf16), 4)
    gate_up = jnp.dot(normed_two_all, in_weights, preferred_element_type=f32)
    gate_part = gate_up[:, :unit_width]
    up_part = gate_up[:, unit_width:]
    sigmoid_gate = jax.nn.sigmoid(gate_part)
    activated = (gate_part * sigmoid_gate * up_part).astype(bf16)
    grad_act = jnp.dot(cotangent_all, down_weights, preferred_element_type=f32)
    grad_gate = grad_act * up_part * sigmoid_gate * (1.0 + gate_part * (1.0 - sigmoid_gate))
    grad_up = grad_act * gate_part * sigmoid_gate
    grad_gate_up = jnp.concatenate([grad_gate, grad_up], axis=1).astype(bf16)
    grad_normed_two = scatter_tokens(contract_cols(grad_gate_up, in_weights), 5)

    def reduce_rows(term):
        return lax.psum_scatter(term.astype(bf16), "fsdp", scatter_dimension=0, tiled=True)

    def collect_rows(total, parts, width):
        moved = lax.all_to_all(
            total.reshape(groups, owned_rows, parts, width),
            "seq",
            split_axis=0,
            concat_axis=0,
            tiled=True,
        ).astype(f32)
        return moved.transpose(1, 2, 0, 3).reshape(owned_rows, parts * groups * width)

    down_sum = reduce_rows(contract_rows(cotangent_all, activated))
    in_sum = reduce_rows(contract_rows(normed_two_all, grad_gate_up))

    grad_hidden = upstream + norm_backward(grad_normed_two, normal_two, inverse_two, gain_two)
    grad_gain_two = jnp.sum(grad_normed_two * normal_two, axis=0)
    grad_shift_two = jnp.sum(grad_normed_two, axis=0)
    grad_hidden_all = gather_tokens(grad_hidden.astype(bf16), 6)
    grad_heads = (
        contract_cols(grad_hidden_all, out_weights).astype(bf16).reshape(length, local_heads, HD)
    )
    out_sum = reduce_rows(contract_rows(attended, grad_hidden_all))
    result = hidden + scatter_tokens(contract_cols(activated, down_weights), 7)

    def backward_block(carry, items):
        grad_key_sum, grad_value_sum = carry
        start_row, logsum_block = items
        query_block = lax.dynamic_slice_in_dim(query_all, start_row, block_rows)
        output_block = lax.dynamic_slice_in_dim(output_heads, start_row, block_rows)
        grad_block = lax.dynamic_slice_in_dim(grad_heads, start_row, block_rows)
        scores = (
            jnp.einsum("bhd,lhd->hbl", query_block, key_all, preferred_element_type=jnp.float32)
            * score_scale
        )
        scores = jnp.where(block_mask(segment_ids, start_row, block_rows)[None], scores, neg_fill)
        probability = jnp.exp(scores - logsum_block[..., None])
        prob_low = probability.astype(jnp.bfloat16)
        grad_value_sum = grad_value_sum + jnp.einsum(
            "hbl,bhd->lhd", prob_low, grad_block, preferred_element_type=jnp.float32
        )
        grad_prob = jnp.einsum(
            "bhd,lhd->hbl", grad_block, value_all, preferred_element_type=jnp.float32
        )
        row_delta = jnp.sum(
            grad_block.astype(jnp.float32) * output_block.astype(jnp.float32), axis=-1
        )
        row_delta = jnp.transpose(row_delta)[..., None]
        grad_scores = (probability * (grad_prob - row_delta) * score_scale).astype(jnp.bfloat16)
        grad_query = jnp.einsum(
            "hbl,lhd->bhd", grad_scores, key_all, preferred_element_type=jnp.float32
        ).astype(jnp.bfloat16)
        grad_key_sum = grad_key_sum + jnp.einsum(
            "hbl,bhd->lhd", grad_scores, query_block, preferred_element_type=jnp.float32
        )
        return ((grad_key_sum, grad_value_sum), grad_query)

    zero_heads = jnp.zeros((length, local_heads, HD), jnp.float32)
    sums, grad_query_blocks = lax.scan(
        backward_block, (zero_heads, zero_heads), (block_starts, logsum_blocks)
    )
    grad_key_sum, grad_value_sum = sums
    grad_query_low = grad_query_blocks.reshape(length, local_heads, HD)
    grad_projected = jnp.concatenate(
        [
            rotate(grad_query_low.astype(f32), cosine, sine, half_rot, -1.0).reshape(
                length, local_width
            ),
            rotate(
                lax.optimization_barrier(grad_key_sum.astype(bf16)).astype(f32),
                cosine,
                sine,
                half_rot,
                -1.0,
            ).reshape(length, local_width),
            lax.optimization_barrier(grad_value_sum.astype(bf16)).astype(f32).reshape(
                length, local_width
            ),
        ],
        axis=1,
    )
    grad_bias = jnp.sum(grad_projected, axis=0)
    grad_projected_low = grad_projected.astype(bf16)
    qkv_sum = reduce_rows(contract_rows(normed_all, grad_projected_low))
    grad_normed_one = scatter_tokens(contract_cols(grad_projected_low, qkv_weights), 8)
    grad_stream = grad_hidden + norm_backward(grad_normed_one, normal_one, inverse_one, gain_one)
    grad_gain_one = jnp.sum(grad_normed_one * normal_one, axis=0)
    grad_shift_one = jnp.sum(grad_normed_one, axis=0)

    feedforward_grad = jnp.concatenate(
        [collect_rows(in_sum, 2, unit_width), collect_rows(down_sum, 1, unit_width)], axis=1
    )
    attention_grad = jnp.concatenate(
        [collect_rows(qkv_sum, 3, local_width), from_order(out_sum.astype(f32))], axis=1
    )
    bias_rows = lax.dynamic_update_slice_in_dim(
        jnp.zeros((3, D), f32), grad_bias.reshape(3, local_width), my_rank * local_width, axis=1
    )
    vector_term = jnp.concatenate(
        [
            from_order(jnp.stack([grad_gain_one, grad_shift_one])),
            bias_rows,
            from_order(jnp.stack([grad_gain_two, grad_shift_two])),
        ]
    )
    vector_grad = lax.psum_scatter(vector_term, ("seq", "fsdp"), scatter_dimension=1, tiled=True)
    attention_new, attention_state = adamw_update(
        attention_weights, attention_grad, attention_moments, decay_rate
    )
    feedforward_new, feedforward_state = adamw_update(
        feedforward_weights, feedforward_grad, feedforward_moments, decay_rate
    )
    vector_new, vector_state = adamw_update(norm_vectors, vector_grad, vector_moments, 0.0)
    return (
        from_order(result)[None],
        from_order(grad_stream)[None],
        attention_grad,
        feedforward_grad,
        vector_grad,
        attention_new,
        feedforward_new,
        vector_new,
        attention_state,
        feedforward_state,
        vector_state,
    )


def solution(mesh):
    in_specs = (
        P("fsdp", "seq", None),
        P("fsdp", None),
        P(("seq", "fsdp"), None),
        P(("seq", "fsdp"), None),
        P(None, ("seq", "fsdp")),
        P(None, ("seq", "fsdp"), None),
        P(None, ("seq", "fsdp"), None),
        P(None, None, ("seq", "fsdp")),
        P("fsdp", "seq", None),
    )
    out_specs = (
        P("fsdp", "seq", None),
        P("fsdp", "seq", None),
        P(("seq", "fsdp"), None),
        P(("seq", "fsdp"), None),
        P(None, ("seq", "fsdp")),
        P(("seq", "fsdp"), None),
        P(("seq", "fsdp"), None),
        P(None, ("seq", "fsdp")),
        P(None, ("seq", "fsdp"), None),
        P(None, ("seq", "fsdp"), None),
        P(None, None, ("seq", "fsdp")),
    )
    return jax.shard_map(body, mesh=mesh, in_specs=in_specs, out_specs=out_specs, check_vma=False)
```

time: 1560 us -> 855 us (0.55)
  waiting for transfers between devices: 1000 us -> 255 us
  Pallas kernels: 0 us -> 191 us
  local copies, waits for them, and re-layouts: 180 us -> 79.6 us
  matrix products: 176 us -> 113 us
  blocking collectives: 73.3 us -> 113 us
    all_gather x6 -> x4, waiting for transfers between devices: 428 us -> 0.06 us  [the longest x1 0.02 us: body(): lax.all_gather(to_order(attention_low[:, 3 * D:]), 'fsdp', axis=0, tiled=...]
    reduce_scatter x2 -> x4, waiting for transfers between devices: 347 us -> 114 us  [reduce_rows(): lax.psum_scatter(term.astype(bf16), 'fsdp', scatter_dimension=0, tiled=True)]
    pallas_call x0 -> x8, Pallas kernels: none -> 191 us  [the longest x4 103 us: plane_gather(): pl.pallas_call(gather_kernel, out_shape=jax.ShapeDtypeStruct((8, rows, co...]
    all_to_all x7 -> x4, waiting for transfers between devices: 77.5 us -> 20 us  [the longest x3 20 us: collect_rows(): lax.all_to_all(total.reshape(groups, owned_rows, parts, width), 'seq', sp...]
    reshape x8 -> x23, local copies, waits for them, and re-layouts: 85.9 us -> 33.3 us  [the longest x5 10.1 us: spread_columns(): values.reshape(owned_rows, parts, groups, width).transpose(2, 0, 1, 3)]
    all_to_all x0 -> x2, blocking collectives: none -> 41.4 us  [spread_columns(): lax.all_to_all(blocks, 'seq', split_axis=0, concat_axis=0, tiled=True)]
    dot_general x4, matrix products: 57.9 us -> 25 us  [contract_cols(): lax.dot_general(left, right, (((1,), (1,)), ((), ())), preferred_element_...]
    unnamed x12 -> x10, waiting for transfers between devices: 148 us -> 121 us
  transfers between devices with their start and end apart: 17 -> 13, of which waited for: 13 -> 6; matrix products, arithmetic and copies ran while one was open for 24% -> 21% of each run, Pallas kernels for 0% -> 20%
where the time goes in v1:
time: 855 us; the launch traced here: 845 us
  waiting for transfers between devices  255 us (30%)
  Pallas kernels  191 us (22%)
  blocking collectives  113 us (13%)
  matrix products  113 us (13%)
  local copies, waits for them, and re-layouts  79.6 us (9%)
  other arithmetic  51.6 us (6%)
  starting transfers between devices  18.3 us (2%)
  between operations  15.3 us (2%)
    unnamed x10, waiting for transfers between devices  121 us
    reduce_scatter x4, waiting for transfers between devices, reduce_rows(): lax.psum_scatter(term.astype(bf16), 'fsdp', scatter_dimension=0, tiled=True)  114 us
    pallas_call x4, Pallas kernels, plane_gather(): pl.pallas_call(gather_kernel, out_shape=jax.ShapeDtypeStruct((8, rows, co...  103 us
    pallas_call x4, Pallas kernels, plane_scatter(): pl.pallas_call(scatter_kernel, out_shape=jax.ShapeDtypeStruct((rows, cols...  88.4 us
    all_gather x1, blocking collectives, body(): lax.all_gather(norm_vectors.astype(bf16), ('seq', 'fsdp'), axis=1, tiled=...  71.3 us
    all_to_all x2, blocking collectives, spread_columns(): lax.all_to_all(blocks, 'seq', split_axis=0, concat_axis=0, tiled=True)  41.4 us
    dot_general x4, matrix products, contract_rows(): lax.dot_general(left, right, (((0,), (0,)), ((), ())), preferred_element_...  25.3 us
    dot_general x4, matrix products, contract_cols(): lax.dot_general(left, right, (((1,), (1,)), ((), ())), preferred_element_...  25 us
  transfers between devices with their start and end apart: 13, of which 6 were waited for; matrix products, arithmetic and copies ran while one was open for 21% of the time, Pallas kernels for 20%

profile of v1, /device:TPU:0, one launch (start us, length us, event | category | flops | bytes accessed | tf_op | source)
XLA Modules:
  0.0 844.7 jit_solution(14931035129347185042)
XLA Ops:
  10.5 17.6 %all_to_all.30 = bf16[8,64,768]{2,1,0:T(8,128)(2,1)} all-to-all(bf16[8,64,768]{2,1,0:T(8,128)(2,1)S(1)} %reshape.651), channel_id=1, replica_groups=mesh['seq'=8,'fsdp'=4] {'seq'}, dimensions={0} | all-to-all | bytes 1572864 | tf_op jit(solution)/shard_map/all_to_all | solution.py:309
  33.7 4.3 reshape.659
  38.0 3.8 copy.226
  41.8 4.7 reshape.660
  46.4 23.8 %all_to_all.31 = bf16[8,64,1408]{2,1,0:T(8,128)(2,1)} all-to-all(bf16[8,64,1408]{2,1,0:T(8,128)(2,1)} %reshape.660), channel_id=1, replica_groups=mesh['seq'=8,'fsdp'=4] {'seq'}, dimensions={0} | all-to-all | bytes 2883584 | tf_op jit(solution)/shard_map/all_to_all | solution.py:309
  72.0 4.4 all-to-all-start.2
  76.5 71.3 %all-gather = bf16[32,64,7]{1,2,0:T(8,128)(2,1)S(1)} all-gather(bf16[1,64,7]{1,2,0:T(8,128)(2,1)S(1)} %convert_bitcast_fusion.4), channel_id=1, replica_groups=mesh['seq'=8,'fsdp'=4] {'seq','fsdp'}, dimensions={0}, use_global_device_ids=true | all-gather | bytes 29568 | tf_op jit(solution)/shard_map/all_gather | solution.py:314
  155.2 25.2 %plane_gather.4 = bf16[8,128,2048]{2,1,0:T(8,128)(2,1)} custom-call(bf16[128,2048]{1,0:T(8,128)(2,1)} %add_convert_fusion.1.x_ref), custom_call_target="tpu_custom_call" | custom-call | tf_op jit(solution)/shard_map/plane_gather/pallas_call | solution.py:167
  180.4 25.6 %plane_gather.6 = bf16[8,128,2048]{2,1,0:T(8,128)(2,1)} custom-call(bf16[128,2048]{1,0:T(8,128)(2,1)} %convert_element_type.132.x_ref), custom_call_target="tpu_custom_call" | custom-call | tf_op jit(solution)/shard_map/plane_gather/pallas_call | solution.py:167
  207.4 6.2 convolution_add_fusion
  215.0 22.5 %while.27 = (s32[]{:T(128)}, bf16[2,512,4,64]{1,3,2,0:T(8,128)(2,1)S(1)}, f32[2,4,512]{2,1,0:T(4,128)S(1)}, s32[2]{0:T(128)S(1)}, s32[1,1024]{1,0:T(1,128)S(1)},...) while((s32[]{:T(128)}, ...), condition=%wide.region_7.8_spmd, body=%wide.region_4.7_spmd.sunk | while | flops 563739136 | bytes 31013084 | solution.py:363
  223.1 3.1 fusion.126
  234.3 3.1 fusion.126
  239.0 2.7 convolution_convert_fusion.3
  241.7 22.1 %plane_scatter.4 = f32[128,2048]{1,0:T(8,128)S(1)} custom-call(bf16[8,128,2048]{2,1,0:T(8,128)(2,1)S(1)} %bitcast.266), custom_call_target="tpu_custom_call" | custom-call | tf_op jit(solution)/shard_map/plane_scatter/pallas_call | solution.py:237
  265.3 26.3 %plane_gather.5 = bf16[8,128,2048]{2,1,0:T(8,128)(2,1)} custom-call(bf16[128,2048]{1,0:T(8,128)(2,1)} %add_convert_fusion.x_ref), custom_call_target="tpu_custom_call" | custom-call | tf_op jit(solution)/shard_map/plane_gather/pallas_call | solution.py:167
  291.6 12.1 %fusion.72 = f32[1024,1408]{1,0:T(8,128)} fusion(bf16[1024,2048]{1,0:T(8,128)(2,1)} %bitcast.283, bf16[2048,1408]{1,0:T(8,128)(2,1)} %all-gather.10.cloned.1.call-done), kind=kOutput, calls=%fused_computation.189 | convolution fusion | flops 5905580032 | bytes 15728640 | tf_op jit(solution)/shard_map/dot_general | solution.py:369
  303.7 10.9 %multiply_convert_fusion.2 = (bf16[1024,704]{1,0:T(8,128)(2,1)}, bf16[1024,704]{1,0:T(8,128)(2,1)}, bf16[1024,704]{1,0:T(8,128)(2,1)S(1)}) fusion(f32[1024,1408]{1,0:T(8,128)} %fusion.72, bf16[1024,2048]{1,0:T(8,128)(2,1)} %bitcast.287, bf16[2048,704]{1,0:T(8,128)(2,1)} %all-gather.12.cloned.1.call-done), kind=kOutput, calls=%fused_computation.75 | convolution fusion | flops 2964324352 | bytes 17170432 | tf_op jit(solution)/shard_map/dot_general | solution.py:374
  315.8 4.5 fusion.45
  320.3 9.7 %convolution_convert_fusion.2 = bf16[1024,2048]{1,0:T(8,128)(2,1)S(1)} fusion(bf16[2048,1408]{1,0:T(8,128)(2,1)} %all-gather.10.cloned.1.call-done, bf16[1024,704]{1,0:T(8,128)(2,1)} %get-tuple-element.280, bf16[1024,704]{1,0:T(8,128)(2,1)} %get-tuple-element.279), kind=kOutput, calls=%fused_computation.64 | convolution fusion | flops 5913444352 | bytes 12845056 | tf_op jit(solution)/shard_map/dot_general | solution.py:84
  330.0 22.1 %plane_scatter.6 = f32[128,2048]{1,0:T(8,128)S(1)} custom-call(bf16[8,128,2048]{2,1,0:T(8,128)(2,1)S(1)} %bitcast.268), custom_call_target="tpu_custom_call" | custom-call | tf_op jit(solution)/shard_map/plane_scatter/pallas_call | solution.py:237
  352.6 5.8 convolution_convert_fusion.5
  358.4 22.1 %plane_scatter.5 = f32[128,2048]{1,0:T(8,128)S(1)} custom-call(bf16[8,128,2048]{2,1,0:T(8,128)(2,1)S(1)} %bitcast.267), custom_call_target="tpu_custom_call" | custom-call | tf_op jit(solution)/shard_map/plane_scatter/pallas_call | solution.py:237
  382.6 25.4 %plane_gather.7 = bf16[8,128,2048]{2,1,0:T(8,128)(2,1)} custom-call(bf16[128,2048]{1,0:T(8,128)(2,1)} %get-tuple-element.271.x_ref), custom_call_target="tpu_custom_call" | custom-call | tf_op jit(solution)/shard_map/plane_gather/pallas_call | solution.py:167
  408.1 3.9 convolution_convert_fusion.9
  412.8 29.2 %while.28 = (s32[]{:T(128)}, f32[1024,4,64]{0,2,1:T(8,128)S(1)}, f32[1024,4,64]{0,2,1:T(8,128)}, bf16[2,512,4,64]{1,3,2,0:T(8,128)(2,1)}, s32[2]{0:T(128)S(1)}, ...) while((s32[]{:T(128)}, f32[1024,4,64]{0,2,1:T(8,128)S(1)}, ...), condition=%wide.region_14.15_spmd.clone, body=%wide.region_12.14_spmd.clone.sunk | while | flops 1368521216 | bytes 61667716 | solution.py:439
  420.9 3.9 multiply_convert_fusion.5
  435.5 3.9 multiply_convert_fusion.5
  446.5 5.2 convolution_convert_fusion.6
  452.1 5.6 convolution_convert_fusion.4
  457.8 22.1 %plane_scatter.7 = f32[128,2048]{1,0:T(8,128)S(1)} custom-call(bf16[8,128,2048]{2,1,0:T(8,128)(2,1)S(1)} %bitcast.269), custom_call_target="tpu_custom_call" | custom-call | tf_op jit(solution)/shard_map/plane_scatter/pallas_call | solution.py:237
  482.4 4.4 convolution_convert_fusion.8
  486.9 11.2 %convolution_convert_fusion.1 = bf16[2048,1408]{1,0:T(8,128)(2,1)} fusion(bf16[1024,2048]{1,0:T(8,128)(2,1)} %bitcast.284, bf16[1024,704]{1,0:T(8,128)(2,1)} %get-tuple-element.280, bf16[1024,704]{1,0:T(8,128)(2,1)} %get-tuple-element.279), kind=kOutput, calls=%fused_computation.47 | convolution fusion | flops 5914230784 | bytes 12845056 | tf_op jit(solution)/shard_map/dot_general | solution.py:80
  500.4 4.2 all-to-all-start.5
  504.7 4.8 reduce-scatter.8.cloned.1.call-done
  513.1 4.2 all-to-all-done.5
  517.3 4.6 all-to-all-start.3
  521.9 2.7 multiply_add_fusion.2
  528.1 120.9 %reduce-scatter.16.cloned.1.call-done = f32[64,7]{1,0:T(8,128)} async-done(((f32[2048,7]{1,0:T(8,128)}), f32[64,7]{1,0:T(8,128)}) %reduce-scatter.16.cloned.1.call-update) | async-done | bytes 1808
  651.0 24.9 %reduce-scatter.10.cloned.1.call-done = bf16[64,2048]{1,0:T(8,128)(2,1)} async-done(((bf16[256,2048]{1,0:T(8,128)(2,1)}), bf16[64,2048]{1,0:T(8,128)(2,1)}) %reduce-scatter.10.cloned.1.call-update) | async-done | bytes 262160 | tf_op jit(solution)/shard_map/reduce_scatter | solution.py:381
  692.5 2.9 multiply_subtract_fusion.1
  695.4 84.3 %reduce-scatter.12.cloned.1.call-done = bf16[512,1408]{1,0:T(8,128)(2,1)} async-done(((bf16[2048,1408]{1,0:T(8,128)(2,1)}), bf16[512,1408]{1,0:T(8,128)(2,1)}) %reduce-scatter.12.cloned.1.call-update) | async-done | bytes 1441808 | tf_op jit(solution)/shard_map/reduce_scatter | solution.py:381
  779.7 5.0 reshape.683
  784.7 4.5 all-to-all-start.4
  789.1 2.8 multiply_add_fusion.1
  794.3 15.8 %all-to-all-done.4 = bf16[8,64,2,704]{3,2,1,0:T(2,128)(2,1)} async-done(((bf16[8,64,2,704]{3,2,1,0:T(2,128)(2,1)}), bf16[8,64,2,704]{3,2,1,0:T(2,128)(2,1)}, u32[]{:S(2)}, u32[]{:S(2)}) %all-to-all-start.4) | async-done | bytes 1441824 | tf_op jit(solution)/shard_map/all_to_all | solution.py:384
  826.3 6.3 multiply_subtract_fusion
  833.9 4.1 pad_maximum_fusion
  (316 shorter events, 112.5 us)
Async XLA Ops:
  7.2 200.2 %all-gather.6.cloned.1.call-start = ((), (), s32[]{:S(2)}) async-start(), calls=%async_computation.11 | async-start | bytes 3932160 | tf_op jit(solution)/shard_map/all_gather | solution.py:315
  28.2 210.8 %all-gather.8.cloned.1.call-start = ((), (), s32[]{:S(2)}) async-start(), calls=%async_computation.12 | async-start | bytes 1310720 | tf_op jit(solution)/shard_map/all_gather | solution.py:318
  30.0 261.6 %all-gather.10.cloned.1.call-start = ((), (), s32[]{:S(2)}) async-start(), calls=%async_computation.13 | async-start | bytes 7208960 | tf_op jit(solution)/shard_map/all_gather | solution.py:319
  70.3 6.2 copy-start.40
  70.3 77.7 %copy-start.16 = (f32[1,128,2048]{2,1,0:T(8,128)S(1)}, f32[1,128,2048]{2,1,0:T(8,128)}, u32[]{:S(2)}) copy-start(f32[1,128,2048]{2,1,0:T(8,128)} %param.13) | copy-start | bytes 3145732
  71.0 77.5 %copy-start.27 = (s32[1,1024]{1,0:T(1,128)S(1)}, s32[1,1024]{1,0:T(1,128)}, u32[]{:S(2)}) copy-start(s32[1,1024]{1,0:T(1,128)} %param.14) | copy-start | bytes 12292
  72.0 77.4 %copy-start.31 = (f32[1,128,2048]{2,1,0:T(8,128)S(1)}, f32[1,128,2048]{2,1,0:T(8,128)}, u32[]{:S(2)}) copy-start(f32[1,128,2048]{2,1,0:T(8,128)} %param.21) | copy-start | bytes 3145732
  72.0 135.0 %all-to-all-start.2 = ((bf16[8,64,704]{2,1,0:T(8,128)(2,1)}), bf16[8,64,704]{2,1,0:T(8,128)(2,1)}, u32[]{:S(2)}, u32[]{:S(2)}) async-start(bf16[8,64,704]{2,1,0:T(8,128)(2,1)} %bitcast.227), calls=%async_computation.2 | async-start | bytes 1572864 | tf_op jit(solution)/shard_map/all_to_all | solution.py:309
  76.4 227.3 %all-gather.12.cloned.1.call-start = ((), (), s32[]{:S(2)}) async-start(), calls=%async_computation.14 | async-start | bytes 3932160 | tf_op jit(solution)/shard_map/all_gather | solution.py:322
  149.3 4.9 copy-start.36
  150.2 3.9 copy-start.5
  153.8 110.0 %copy-start.1 = (f32[128,2048]{1,0:T(8,128)}, f32[128,2048]{1,0:T(8,128)S(1)}, u32[]{:S(2)}) copy-start(f32[128,2048]{1,0:T(8,128)S(1)} %copy.159) | copy-start | bytes 3145732
  153.8 26.6 %copy-start.42 = (f32[128]{0:T(128)}, f32[128]{0:T(128)S(1)}, u32[]{:S(2)}) copy-start(f32[128]{0:T(128)S(1)} %broadcast_multiply_fusion.6) | copy-start | bytes 1540
  154.1 26.3 %copy-start.45 = (f32[128]{0:T(128)}, f32[128]{0:T(128)S(1)}, u32[]{:S(2)}) copy-start(f32[128]{0:T(128)S(1)} %add_rsqrt_fusion.1) | copy-start | bytes 1540
  207.1 7.7 copy-start.34
  207.1 291.1 %reduce-scatter.14.cloned.1.call-start = ((), (), s32[]{:S(2)}) async-start(), calls=%async_computation.18 | async-start | bytes 3604480 | tf_op jit(solution)/shard_map/reduce_scatter | solution.py:381
  303.7 12.0 %copy-start.15 = (bf16[8,128,2048]{2,1,0:T(8,128)(2,1)S(1)}, bf16[8,128,2048]{2,1,0:T(8,128)(2,1)}, u32[]{:S(2)}) copy-start(bf16[8,128,2048]{2,1,0:T(8,128)(2,1)} %plane_gather.6) | copy-start | bytes 12582916
  352.1 157.4 %reduce-scatter.8.cloned.1.call-start = ((), (), s32[]{:S(2)}) async-start(), calls=%async_computation.15 | async-start | bytes 3932160 | tf_op jit(solution)/shard_map/reduce_scatter | solution.py:381
  358.4 22.1 %copy-start.6 = (f32[128,2048]{1,0:T(8,128)S(1)}, f32[128,2048]{1,0:T(8,128)}, u32[]{:S(2)}) copy-start(f32[128,2048]{1,0:T(8,128)} %copy-done.5) | copy-start | bytes 3145732
  408.0 4.8 copy-start
  408.1 4.7 copy-start.9
  420.9 4.0 copy-start.29
  420.9 4.0 copy-start.24
  435.5 4.0 copy-start.29
  435.5 4.0 copy-start.24
  444.1 7.9 copy-start.17
  444.2 7.8 copy-start.19
  451.7 197.2 %reduce-scatter.16.cloned.1.call-start = ((), (), s32[]{:S(2)}) async-start(), calls=%async_computation.19 | async-start | bytes 1081344
  457.7 22.2 %copy-start.18 = (f32[1024,4,64]{0,2,1:T(8,128)S(1)}, f32[1024,4,64]{0,2,1:T(8,128)}, u32[]{:S(2)}) copy-start(f32[1024,4,64]{0,2,1:T(8,128)} %copy-done.17) | copy-start | bytes 3145732
  457.7 22.2 %copy-start.20 = (f32[1024,4,64]{0,2,1:T(8,128)S(1)}, f32[1024,4,64]{0,2,1:T(8,128)}, u32[]{:S(2)}) copy-start(f32[1024,4,64]{0,2,1:T(8,128)} %copy-done.19) | copy-start | bytes 3145732
  457.7 22.4 %copy-start.2 = (f32[128,2048]{1,0:T(8,128)S(1)}, f32[128,2048]{1,0:T(8,128)}, u32[]{:S(2)}) copy-start(f32[128,2048]{1,0:T(8,128)} %copy-done.1) | copy-start | bytes 3145732
  457.7 22.4 %copy-start.37 = (f32[2048]{0:T(1024)S(1)}, f32[2048]{0:T(1024)}, u32[]{:S(2)}) copy-start(f32[2048]{0:T(1024)} %copy-done.36) | copy-start | bytes 24580
  457.7 22.4 %copy-start.43 = (f32[128]{0:T(128)S(1)}, f32[128]{0:T(128)}, u32[]{:S(2)}) copy-start(f32[128]{0:T(128)} %copy-done.42) | copy-start | bytes 1540
  457.8 22.4 %copy-start.46 = (f32[128]{0:T(128)S(1)}, f32[128]{0:T(128)}, u32[]{:S(2)}) copy-start(f32[128]{0:T(128)} %copy-done.45) | copy-start | bytes 1540
  482.3 193.6 %reduce-scatter.10.cloned.1.call-start = ((), (), s32[]{:S(2)}) async-start(), calls=%async_computation.16 | async-start | bytes 1310720 | tf_op jit(solution)/shard_map/reduce_scatter | solution.py:381
  486.8 292.8 %reduce-scatter.12.cloned.1.call-start = ((), (), s32[]{:S(2)}) async-start(), calls=%async_computation.17 | async-start | bytes 7208960 | tf_op jit(solution)/shard_map/reduce_scatter | solution.py:381
  498.1 6.6 copy-start.44
  500.4 16.8 %all-to-all-start.5 = ((bf16[8,64,1,704]{3,1,2,0:T(8,128)(2,1)}), bf16[8,64,1,704]{3,1,2,0:T(8,128)(2,1)}, u32[]{:S(2)}, u32[]{:S(2)}) async-start(bf16[8,64,1,704]{3,1,2,0:T(8,128)(2,1)} %bitcast.54), calls=%async_computation.9 | async-start | bytes 1572864 | tf_op jit(solution)/shard_map/all_to_all | solution.py:384
  513.1 11.5 %copy-start.13 = (f32[128,2048]{1,0:T(8,128)S(1)}, f32[128,2048]{1,0:T(8,128)}, u32[]{:S(2)}) copy-start(f32[128,2048]{1,0:T(8,128)} %get-tuple-element.294) | copy-start | bytes 3145732
  517.3 167.4 %all-to-all-start.3 = ((bf16[8,64,3,256]{3,1,2,0:T(8,128)(2,1)}), bf16[8,64,3,256]{3,1,2,0:T(8,128)(2,1)}, u32[]{:S(2)}, u32[]{:S(2)}) async-start(bf16[8,64,3,256]{3,1,2,0:T(8,128)(2,1)} %copy.174), calls=%async_computation.4 | async-start | bytes 1572864 | tf_op jit(solution)/shard_map/all_to_all | solution.py:384
  526.3 123.5 %copy-start.41 = (f32[7,64]{1,0:T(8,128)S(1)}, f32[7,64]{1,0:T(8,128)}, u32[]{:S(2)}) copy-start(f32[7,64]{1,0:T(8,128)} %param.17) | copy-start | bytes 5380
  649.8 29.3 %copy-start.39 = (f32[7,64]{1,0:T(8,128)}, f32[7,64]{1,0:T(8,128)S(1)}, u32[]{:S(2)}) copy-start(f32[7,64]{1,0:T(8,128)S(1)} %copy.194) | copy-start | bytes 5380
  784.7 25.5 %all-to-all-start.4 = ((bf16[8,64,2,704]{3,2,1,0:T(2,128)(2,1)}), bf16[8,64,2,704]{3,2,1,0:T(2,128)(2,1)}, u32[]{:S(2)}, u32[]{:S(2)}) async-start(bf16[8,64,2,704]{3,2,1,0:T(2,128)(2,1)} %reshape.683), calls=%async_computation.7 | async-start | bytes 3145728 | tf_op jit(solution)/shard_map/all_to_all | solution.py:384
  817.1 7.6 slice-start
  819.7 4.8 copy-start.12
  819.7 5.0 slice-start.1
  821.9 4.4 slice-start.2
  824.6 8.0 copy-start.4
  (22 other events, 40.7 us)
Sparse Core Ops, SparseCore 0:
  28.3 62.9 all-gather.5
  93.5 27.0 all-gather.7
  122.1 106.0 all-gather.9
  229.7 61.7 all-gather.11
  352.2 53.5 reduce-scatter.13
  451.8 57.6 reduce-scatter.7
  511.8 137.1 reduce-scatter.15
  651.8 24.0 reduce-scatter.9
  678.8 100.7 reduce-scatter.11

commit v2 on v1

--- a/solution.py
+++ b/solution.py
@@ -1,5 +1,3 @@
-import functools
-
 import jax
 import jax.numpy as jnp
 from jax import lax
@@ -24,6 +22,7 @@
 adam_step = 2.0
 
 MESH_IDS = pl.DeviceIdType.MESH
+BOTH = ("seq", "fsdp")
 bf16 = jnp.bfloat16
 f32 = jnp.float32
 
@@ -118,7 +117,7 @@
 def greet(others):
     barrier = pltpu.get_barrier_semaphore()
     for other in others:
-        pl.semaphore_signal(barrier, inc=1, device_id={"seq": other}, device_id_type=MESH_IDS)
+        pl.semaphore_signal(barrier, inc=1, device_id=other, device_id_type=MESH_IDS)
     pl.semaphore_wait(barrier, len(others))
 
 
@@ -135,7 +134,7 @@
             device_id_type=MESH_IDS,
         )
 
-    greet((sibling, near, far))
+    greet([{"seq": other} for other in (sibling, near, far)])
     own = pltpu.make_async_copy(x_ref, o_ref.at[me], local_sem)
     own.start()
     to_near = copy(x_ref, me, 0, near)
@@ -196,7 +195,7 @@
             device_id_type=MESH_IDS,
         )
 
-    greet((sibling, near, far))
+    greet([{"seq": other} for other in (sibling, near, far)])
     pairs = []
     locals_ = []
     for index, block in enumerate(order):
@@ -257,6 +256,137 @@
     )(values.reshape(8, rows, cols))
 
 
+def peers(axis, size):
+    me = lax.axis_index(axis)
+    others = tuple((me + k) % size for k in range(1, size))
+    return me, others
+
+
+def vector_gather_kernel(x_ref, o_ref, send_sem, recv_sem):
+    seq, seq_others = peers("seq", 8)
+    fsdp, fsdp_others = peers("fsdp", 4)
+    greet([{"fsdp": other} for other in fsdp_others] + [{"seq": other} for other in seq_others])
+    o_ref[seq, fsdp] = x_ref[...]
+    copies = []
+    for k, other in enumerate(fsdp_others):
+        copies.append(
+            pltpu.make_async_remote_copy(
+                src_ref=x_ref,
+                dst_ref=o_ref.at[seq, fsdp],
+                send_sem=send_sem.at[k],
+                recv_sem=recv_sem.at[k],
+                device_id={"fsdp": other},
+                device_id_type=MESH_IDS,
+            )
+        )
+        copies[-1].start()
+    for one in copies:
+        one.wait_recv()
+    for k, other in enumerate(seq_others):
+        copies.append(
+            pltpu.make_async_remote_copy(
+                src_ref=o_ref.at[seq],
+                dst_ref=o_ref.at[seq],
+                send_sem=send_sem.at[3 + k],
+                recv_sem=recv_sem.at[3 + k],
+                device_id={"seq": other},
+                device_id_type=MESH_IDS,
+            )
+        )
+        copies[-1].start()
+    for one in copies[3:]:
+        one.wait_recv()
+    for one in copies:
+        one.wait_send()
+
+
+def vector_sum_kernel(x_ref, o_ref, part, total, last, send_sem, recv_sem):
+    seq, seq_others = peers("seq", 8)
+    _, fsdp_others = peers("fsdp", 4)
+    greet([{"fsdp": other} for other in fsdp_others] + [{"seq": other} for other in seq_others])
+    copies = []
+    for k, other in enumerate(seq_others):
+        copies.append(
+            pltpu.make_async_remote_copy(
+                src_ref=x_ref.at[other],
+                dst_ref=part.at[k],
+                send_sem=send_sem.at[k],
+                recv_sem=recv_sem.at[k],
+                device_id={"seq": other},
+                device_id_type=MESH_IDS,
+            )
+        )
+        copies[-1].start()
+    for one in copies:
+        one.wait_recv()
+    total[...] = x_ref[seq] + jnp.sum(part[...], axis=0)
+    for k, other in enumerate(fsdp_others):
+        copies.append(
+            pltpu.make_async_remote_copy(
+                src_ref=total,
+                dst_ref=last.at[k],
+                send_sem=send_sem.at[7 + k],
+                recv_sem=recv_sem.at[7 + k],
+                device_id={"fsdp": other},
+                device_id_type=MESH_IDS,
+            )
+        )
+        copies[-1].start()
+    for one in copies[7:]:
+        one.wait_recv()
+    o_ref[...] = total[...] + jnp.sum(last[...], axis=0)
+    for one in copies:
+        one.wait_send()
+
+
+def gather_vectors(values, collective_id):
+    rows = values.shape[1]
+    if on_grid():
+        padded = jnp.pad(values.astype(f32), ((0, 1), (0, 128 - rows)))
+        out = pl.pallas_call(
+            vector_gather_kernel,
+            out_shape=jax.ShapeDtypeStruct((8, 4, 8, 128), f32),
+            in_specs=[pl.BlockSpec(memory_space=pltpu.VMEM)],
+            out_specs=pl.BlockSpec(memory_space=pltpu.VMEM),
+            scratch_shapes=[pltpu.SemaphoreType.DMA((10,)), pltpu.SemaphoreType.DMA((10,))],
+            compiler_params=pltpu.CompilerParams(collective_id=collective_id, has_side_effects=True),
+            name="vector_gather",
+        )(padded)
+        return out[:, :, :7, :rows].transpose(2, 0, 1, 3).reshape(7, D)
+    return lax.all_gather(values, BOTH, axis=1, tiled=True).astype(f32)
+
+
+def sum_vectors(values, collective_id):
+    if on_grid():
+        blocks = jnp.pad(values.reshape(7, 8, D // 8).transpose(1, 0, 2), ((0, 0), (0, 1), (0, 0)))
+        out = pl.pallas_call(
+            vector_sum_kernel,
+            out_shape=jax.ShapeDtypeStruct((8, D // 8), f32),
+            in_specs=[pl.BlockSpec(memory_space=pltpu.VMEM)],
+            out_specs=pl.BlockSpec(memory_space=pltpu.VMEM),
+            scratch_shapes=[
+                pltpu.VMEM((7, 8, D // 8), f32),
+                pltpu.VMEM((8, D // 8), f32),
+                pltpu.VMEM((3, 8, D // 8), f32),
+                pltpu.SemaphoreType.DMA((10,)),
+                pltpu.SemaphoreType.DMA((10,)),
+            ],
+            compiler_params=pltpu.CompilerParams(collective_id=collective_id, has_side_effects=True),
+            name="vector_sum",
+        )(blocks)
+        rows = D // 32
+        return lax.dynamic_slice_in_dim(out[:7], lax.axis_index("fsdp") * rows, rows, axis=1)
+    return lax.psum_scatter(values, BOTH, scatter_dimension=1, tiled=True)
+
+
+def on_grid():
+    return lax.axis_size("seq") == 8 and lax.axis_size("fsdp") == 4
+
+
+def after(values, *others):
+    return lax.optimization_barrier((values, *others))[0]
+
+
 def gather_tokens(values, collective_id):
     if lax.axis_size("seq") == 8:
         return plane_gather(values, collective_id)
@@ -309,21 +439,18 @@
         moved = lax.all_to_all(blocks, "seq", split_axis=0, concat_axis=0, tiled=True)
         return moved.reshape(plane_rows, parts * width)
 
+    vector_full = gather_vectors(norm_vectors.astype(bf16), 9)
     attention_low = attention_weights.astype(bf16)
     feedforward_low = feedforward_weights.astype(bf16)
-    vector_low = lax.all_gather(norm_vectors.astype(bf16), ("seq", "fsdp"), axis=1, tiled=True)
-    qkv_weights = lax.all_gather(
-        spread_columns(attention_low[:, : 3 * D], 3, local_width), "fsdp", axis=0, tiled=True
-    )
-    out_weights = lax.all_gather(to_order(attention_low[:, 3 * D :]), "fsdp", axis=0, tiled=True)
-    in_weights = lax.all_gather(
-        spread_columns(feedforward_low[:, : 2 * FF], 2, unit_width), "fsdp", axis=0, tiled=True
-    )
-    down_weights = lax.all_gather(
-        spread_columns(feedforward_low[:, 2 * FF :], 1, unit_width), "fsdp", axis=0, tiled=True
-    )
-
-    vector_full = vector_low.astype(f32)
+    out_weights = lax.all_gather(attention_low[:, 3 * D :], "fsdp", axis=0, tiled=True)
+    out_weights = to_order(out_weights)
+    qkv_block = spread_columns(attention_low[:, : 3 * D], 3, local_width)
+    qkv_weights = lax.all_gather(qkv_block, "fsdp", axis=0, tiled=True)
+    down_block = spread_columns(feedforward_low[:, 2 * FF :], 1, unit_width)
+    down_weights = lax.all_gather(down_block, "fsdp", axis=0, tiled=True)
+    in_block = spread_columns(feedforward_low[:, : 2 * FF], 2, unit_width)
+    in_weights = lax.all_gather(in_block, "fsdp", axis=0, tiled=True)
+
     ordered = to_order(vector_full)
     gain_one, shift_one, gain_two, shift_two = [ordered[i] for i in (0, 1, 5, 6)]
     bias = lax.dynamic_slice_in_dim(
@@ -366,19 +493,18 @@
     hidden = inputs + scatter_tokens(jnp.dot(attended, out_weights, preferred_element_type=f32), 3)
     normed_two, normal_two, inverse_two = norm_forward(hidden, gain_two, shift_two)
     normed_two_all = gather_tokens(normed_two.astype(bf16), 4)
+    grad_act = jnp.dot(cotangent_all, down_weights, preferred_element_type=f32)
     gate_up = jnp.dot(normed_two_all, in_weights, preferred_element_type=f32)
     gate_part = gate_up[:, :unit_width]
     up_part = gate_up[:, unit_width:]
     sigmoid_gate = jax.nn.sigmoid(gate_part)
     activated = (gate_part * sigmoid_gate * up_part).astype(bf16)
-    grad_act = jnp.dot(cotangent_all, down_weights, preferred_element_type=f32)
     grad_gate = grad_act * up_part * sigmoid_gate * (1.0 + gate_part * (1.0 - sigmoid_gate))
     grad_up = grad_act * gate_part * sigmoid_gate
     grad_gate_up = jnp.concatenate([grad_gate, grad_up], axis=1).astype(bf16)
-    grad_normed_two = scatter_tokens(contract_cols(grad_gate_up, in_weights), 5)
 
     def reduce_rows(term):
-        return lax.psum_scatter(term.astype(bf16), "fsdp", scatter_dimension=0, tiled=True)
+        return lax.psum_scatter(term, "fsdp", scatter_dimension=0, tiled=True)
 
     def collect_rows(total, parts, width):
         moved = lax.all_to_all(
@@ -390,8 +516,13 @@
         ).astype(f32)
         return moved.transpose(1, 2, 0, 3).reshape(owned_rows, parts * groups * width)
 
-    down_sum = reduce_rows(contract_rows(cotangent_all, activated))
-    in_sum = reduce_rows(contract_rows(normed_two_all, grad_gate_up))
+    down_term = contract_rows(cotangent_all, activated).astype(bf16)
+    down_sum = reduce_rows(down_term)
+    in_term = contract_rows(normed_two_all, after(grad_gate_up, down_term)).astype(bf16)
+    in_sum = reduce_rows(in_term)
+    grad_normed_two = scatter_tokens(
+        contract_cols(after(grad_gate_up, in_term), in_weights), 5
+    )
 
     grad_hidden = upstream + norm_backward(grad_normed_two, normal_two, inverse_two, gain_two)
     grad_gain_two = jnp.sum(grad_normed_two * normal_two, axis=0)
@@ -400,8 +531,6 @@
     grad_heads = (
         contract_cols(grad_hidden_all, out_weights).astype(bf16).reshape(length, local_heads, HD)
     )
-    out_sum = reduce_rows(contract_rows(attended, grad_hidden_all))
-    result = hidden + scatter_tokens(contract_cols(activated, down_weights), 7)
 
     def backward_block(carry, items):
         grad_key_sum, grad_value_sum = carry
@@ -461,8 +590,16 @@
     )
     grad_bias = jnp.sum(grad_projected, axis=0)
     grad_projected_low = grad_projected.astype(bf16)
-    qkv_sum = reduce_rows(contract_rows(normed_all, grad_projected_low))
-    grad_normed_one = scatter_tokens(contract_cols(grad_projected_low, qkv_weights), 8)
+    qkv_term = contract_rows(normed_all, grad_projected_low).astype(bf16)
+    qkv_sum = reduce_rows(qkv_term)
+    out_term = contract_rows(attended, after(grad_hidden_all, qkv_term)).astype(bf16)
+    out_sum = reduce_rows(out_term)
+    grad_normed_one = scatter_tokens(
+        contract_cols(after(grad_projected_low, out_term), qkv_weights), 8
+    )
+    result = hidden + scatter_tokens(
+        contract_cols(after(activated, grad_normed_one), down_weights), 7
+    )
     grad_stream = grad_hidden + norm_backward(grad_normed_one, normal_one, inverse_one, gain_one)
     grad_gain_one = jnp.sum(grad_normed_one * normal_one, axis=0)
     grad_shift_one = jnp.sum(grad_normed_one, axis=0)
@@ -483,7 +620,7 @@
             from_order(jnp.stack([grad_gain_two, grad_shift_two])),
         ]
     )
-    vector_grad = lax.psum_scatter(vector_term, ("seq", "fsdp"), scatter_dimension=1, tiled=True)
+    vector_grad = sum_vectors(vector_term, 10)
     attention_new, attention_state = adamw_update(
         attention_weights, attention_grad, attention_moments, decay_rate
     )
@@ -531,4 +668,5 @@
         P(None, ("seq", "fsdp"), None),
         P(None, None, ("seq", "fsdp")),
     )
+
     return jax.shard_map(body, mesh=mesh, in_specs=in_specs, out_specs=out_specs, check_vma=False)

time: 855 us -> 680 us (0.80)
  waiting for transfers between devices: 255 us -> 102 us
  blocking collectives: 113 us -> 41.5 us
  Pallas kernels: 191 us -> 226 us
    unnamed x10 -> x8, waiting for transfers between devices: 121 us -> 0.6 us
    all_gather x1 -> x0, blocking collectives: 71.3 us -> none  [body(): lax.all_gather(norm_vectors.astype(bf16), ('seq', 'fsdp'), axis=1, tiled=...]
    reduce_scatter x4, waiting for transfers between devices: 114 us -> 61.1 us  [reduce_rows(): return lax.psum_scatter(term, 'fsdp', scatter_dimension=0, tiled=True)]
    pallas_call x0 -> x2, Pallas kernels: none -> 29.1 us  [the longest x1 16.2 us: sum_vectors(): pl.pallas_call(vector_sum_kernel, out_shape=jax.ShapeDtypeStruct((8, D //...]
    all_gather x4, waiting for transfers between devices: 0.06 us -> 24.1 us  [the longest x1 24 us: body(): down_weights = lax.all_gather(down_block, 'fsdp', axis=0, tiled=True)]
    unnamed x104 -> x98, local copies, waits for them, and re-layouts: 21.5 us -> 24.6 us
  transfers between devices with their start and end apart: 13 -> 12, of which waited for: 6 -> 3; matrix products, arithmetic and copies ran while one was open for 21% -> 29% of each run, Pallas kernels for 20% -> 34%
where the time goes in v2:
time: 680 us; the launch traced here: 670 us
  Pallas kernels  226 us (33%)
  matrix products  113 us (17%)
  waiting for transfers between devices  102 us (15%)
  local copies, waits for them, and re-layouts  87.9 us (13%)
  other arithmetic  58.3 us (9%)
  blocking collectives  41.5 us (6%)
  starting transfers between devices  18 us (3%)
  between operations  15.5 us (2%)
  loops' own time  8.34 us (1%)
    pallas_call x4, Pallas kernels, plane_gather(): pl.pallas_call(gather_kernel, out_shape=jax.ShapeDtypeStruct((8, rows, co...  103 us
    pallas_call x4, Pallas kernels, plane_scatter(): pl.pallas_call(scatter_kernel, out_shape=jax.ShapeDtypeStruct((rows, cols...  93.5 us
    reduce_scatter x4, waiting for transfers between devices, reduce_rows(): return lax.psum_scatter(term, 'fsdp', scatter_dimension=0, tiled=True)  61.1 us
    all_to_all x2, blocking collectives, spread_columns(): lax.all_to_all(blocks, 'seq', split_axis=0, concat_axis=0, tiled=True)  41.5 us
    dot_general x4, matrix products, contract_cols(): lax.dot_general(left, right, (((1,), (1,)), ((), ())), preferred_element_...  27.9 us
    unnamed x98, local copies, waits for them, and re-layouts  24.6 us
    all_gather x1, waiting for transfers between devices, body(): down_weights = lax.all_gather(down_block, 'fsdp', axis=0, tiled=True)  24 us
    dot_general x4, matrix products, contract_rows(): lax.dot_general(left, right, (((0,), (0,)), ((), ())), preferred_element_...  23 us
  transfers between devices with their start and end apart: 12, of which 3 were waited for; matrix products, arithmetic and copies ran while one was open for 29% of the time, Pallas kernels for 34%

profile of v2, /device:TPU:0, one launch (start us, length us, event | category | flops | bytes accessed | tf_op | source)
XLA Modules:
  0.0 670.3 jit_solution(5924823080063956984)
XLA Ops:
  11.3 17.6 %all_to_all.30 = bf16[8,64,768]{2,1,0:T(8,128)(2,1)} all-to-all(bf16[8,64,768]{2,1,0:T(8,128)(2,1)S(1)} %reshape.651), channel_id=1, replica_groups=mesh['seq'=8,'fsdp'=4] {'seq'}, dimensions={0} | all-to-all | bytes 1572864 | tf_op jit(solution)/shard_map/all_to_all | solution.py:439
  32.7 4.2 reshape.659
  36.9 3.8 copy.194
  40.6 4.6 reshape.660
  45.3 23.8 %all_to_all.31 = bf16[8,64,1408]{2,1,0:T(8,128)(2,1)} all-to-all(bf16[8,64,1408]{2,1,0:T(8,128)(2,1)} %reshape.660), channel_id=1, replica_groups=mesh['seq'=8,'fsdp'=4] {'seq'}, dimensions={0} | all-to-all | bytes 2883584 | tf_op jit(solution)/shard_map/all_to_all | solution.py:439
  73.0 4.2 all-to-all-start.2
  78.9 12.9 %vector_gather.1 = f32[8,4,8,128]{3,2,1,0:T(8,128)} custom-call(f32[8,128]{1,0:T(8,128)} %pad_convert_fusion.x_ref), custom_call_target="tpu_custom_call" | custom-call | tf_op jit(solution)/shard_map/vector_gather/pallas_call | solution.py:346
  100.3 25.8 %plane_gather.4 = bf16[8,128,2048]{2,1,0:T(8,128)(2,1)} custom-call(bf16[128,2048]{1,0:T(8,128)(2,1)} %add_convert_fusion.1.x_ref), custom_call_target="tpu_custom_call" | custom-call | tf_op jit(solution)/shard_map/plane_gather/pallas_call | solution.py:166
  126.1 26.2 %plane_gather.6 = bf16[8,128,2048]{2,1,0:T(8,128)(2,1)} custom-call(bf16[128,2048]{1,0:T(8,128)(2,1)} %convert_element_type.132.x_ref), custom_call_target="tpu_custom_call" | custom-call | tf_op jit(solution)/shard_map/plane_gather/pallas_call | solution.py:166
  156.2 6.2 convolution_add_fusion
  163.8 22.3 %while.27 = (s32[]{:T(128)}, bf16[2,512,4,64]{1,3,2,0:T(8,128)(2,1)S(1)}, f32[2,4,512]{2,1,0:T(4,128)S(1)}, s32[2]{0:T(128)S(1)}, s32[1,1024]{1,0:T(1,128)S(1)},...) while((s32[]{:T(128)}, ...), condition=%wide.region_7.8_spmd, body=%wide.region_4.7_spmd.sunk | while | flops 563739136 | bytes 31013084 | solution.py:490
  171.9 3.0 fusion.126
  183.0 3.0 fusion.126
  187.6 2.7 convolution_convert_fusion.3
  190.4 22.1 %plane_scatter.4 = f32[128,2048]{1,0:T(8,128)S(1)} custom-call(bf16[8,128,2048]{2,1,0:T(8,128)(2,1)S(1)} %bitcast.269), custom_call_target="tpu_custom_call" | custom-call | tf_op jit(solution)/shard_map/plane_scatter/pallas_call | solution.py:236
  214.0 25.7 %plane_gather.5 = bf16[8,128,2048]{2,1,0:T(8,128)(2,1)} custom-call(bf16[128,2048]{1,0:T(8,128)(2,1)} %add_convert_fusion.x_ref), custom_call_target="tpu_custom_call" | custom-call | tf_op jit(solution)/shard_map/plane_gather/pallas_call | solution.py:166
  239.7 11.9 %fusion.68 = f32[1024,1408]{1,0:T(8,128)} fusion(bf16[1024,2048]{1,0:T(8,128)(2,1)} %bitcast.296, bf16[2048,1408]{1,0:T(8,128)(2,1)} %all-gather.9.cloned.1.call-done), kind=kOutput, calls=%fused_computation.187 | convolution fusion | flops 5905580032 | bytes 15728640 | tf_op jit(solution)/shard_map/dot_general | solution.py:497
  251.6 24.0 %all-gather.11.cloned.1.call-done = bf16[2048,704]{1,0:T(8,128)(2,1)} async-done(((bf16[512,704]{1,0:T(8,128)(2,1)}), bf16[2048,704]{1,0:T(8,128)(2,1)}) %all-gather.11.cloned.1.call-update) | async-done | bytes 2883600 | tf_op jit(solution)/shard_map/all_gather | solution.py:450
  275.6 10.9 %multiply_convert_fusion.2 = (bf16[1024,704]{1,0:T(8,128)(2,1)}, bf16[1024,704]{1,0:T(8,128)(2,1)}, bf16[1024,704]{1,0:T(8,128)(2,1)S(1)}) fusion(f32[1024,1408]{1,0:T(8,128)} %fusion.68, bf16[1024,2048]{1,0:T(8,128)(2,1)} %bitcast.292, bf16[2048,704]{1,0:T(8,128)(2,1)} %all-gather.11.cloned.1.call-done), kind=kOutput, calls=%fused_computation.75 | convolution fusion | flops 2964324352 | bytes 17170432 | tf_op jit(solution)/shard_map/dot_general | solution.py:496
  287.8 4.5 fusion.45
  292.3 2.9 pad_maximum_fusion.3
  296.8 9.1 %convolution_convert_fusion.1 = bf16[2048,1408]{1,0:T(8,128)(2,1)} fusion(bf16[1024,2048]{1,0:T(8,128)(2,1)S(1)} %bitcast.297, bf16[1024,1408]{1,0:T(8,128)(2,1)S(1)} %pad_maximum_fusion.3), kind=kOutput, calls=%fused_computation.47 | convolution fusion | flops 5908463616 | bytes 12845056 | tf_op jit(solution)/shard_map/dot_general | solution.py:79
  305.9 9.6 %convolution_convert_fusion.2 = bf16[1024,2048]{1,0:T(8,128)(2,1)S(1)} fusion(bf16[1024,1408]{1,0:T(8,128)(2,1)} %copy-done.21, bf16[2048,1408]{1,0:T(8,128)(2,1)} %all-gather.9.cloned.1.call-done), kind=kOutput, calls=%fused_computation.64 | convolution fusion | flops 5907677184 | bytes 12845056 | tf_op jit(solution)/shard_map/dot_general | solution.py:83
  315.5 23.0 %plane_scatter.5 = f32[128,2048]{1,0:T(8,128)S(1)} custom-call(bf16[8,128,2048]{2,1,0:T(8,128)(2,1)S(1)} %bitcast.271), custom_call_target="tpu_custom_call" | custom-call | tf_op jit(solution)/shard_map/plane_scatter/pallas_call | solution.py:236
  340.6 25.4 %plane_gather.7 = bf16[8,128,2048]{2,1,0:T(8,128)(2,1)} custom-call(bf16[128,2048]{1,0:T(8,128)(2,1)} %get-tuple-element.283.x_ref), custom_call_target="tpu_custom_call" | custom-call | tf_op jit(solution)/shard_map/plane_gather/pallas_call | solution.py:166
  366.0 4.7 convolution_convert_fusion.9
  371.5 31.4 %while.28 = (s32[]{:T(128)}, f32[1024,4,64]{0,2,1:T(8,128)S(1)}, f32[1024,4,64]{0,2,1:T(8,128)}, bf16[2,512,4,64]{1,3,2,0:T(8,128)(2,1)}, s32[2]{0:T(128)S(1)}, ...) while((s32[]{:T(128)}, f32[1024,4,64]{0,2,1:T(8,128)S(1)}, ...), condition=%wide.region_14.15_spmd.clone, body=%wide.region_12.14_spmd.clone.sunk | while | flops 1368521216 | bytes 63764896 | solution.py:568
  380.8 3.9 multiply_convert_fusion.5
  396.4 3.9 multiply_convert_fusion.5
  407.9 4.9 convolution_convert_fusion.6
  412.9 4.6 convolution_convert_fusion.8
  420.0 5.8 convolution_convert_fusion.5
  425.9 22.1 %plane_scatter.6 = f32[128,2048]{1,0:T(8,128)S(1)} custom-call(bf16[8,128,2048]{2,1,0:T(8,128)(2,1)S(1)} %bitcast.272), custom_call_target="tpu_custom_call" | custom-call | tf_op jit(solution)/shard_map/plane_scatter/pallas_call | solution.py:236
  448.8 7.8 %convolution_convert_fusion.4 = bf16[1024,2048]{1,0:T(8,128)(2,1)} fusion(bf16[1024,704]{1,0:T(8,128)(2,1)} %copy-done.46, bf16[2048,704]{1,0:T(8,128)(2,1)} %all-gather.11.cloned.1.call-done), kind=kOutput, calls=%fused_computation.66 | convolution fusion | flops 2954887168 | bytes 8519680 | tf_op jit(solution)/shard_map/dot_general | solution.py:83
  458.9 4.2 all-to-all-start.5
  463.8 16.2 %vector_sum.1 = f32[8,256]{1,0:T(8,128)} custom-call(f32[8,8,256]{2,1,0:T(8,128)} %pad.12.x_ref), custom_call_target="tpu_custom_call" | custom-call | tf_op jit(solution)/shard_map/vector_sum/pallas_call | solution.py:362
  480.0 2.7 multiply_add_fusion.2
  486.2 4.6 all-to-all-start.3
  493.2 26.3 %plane_scatter.7 = f32[128,2048]{1,0:T(8,128)S(1)} custom-call(bf16[8,128,2048]{2,1,0:T(8,128)(2,1)S(1)} %bitcast.270), custom_call_target="tpu_custom_call" | custom-call | tf_op jit(solution)/shard_map/plane_scatter/pallas_call | solution.py:236
  541.0 2.9 multiply_subtract_fusion.1
  543.8 61.1 %reduce-scatter.9.cloned.1.call-done = bf16[512,1408]{1,0:T(8,128)(2,1)} async-done(((bf16[2048,1408]{1,0:T(8,128)(2,1)}), bf16[512,1408]{1,0:T(8,128)(2,1)}) %reduce-scatter.9.cloned.1.call-update) | async-done | bytes 1441808 | tf_op jit(solution)/shard_map/reduce_scatter | solution.py:507
  605.0 5.2 reshape.683
  610.1 4.3 all-to-all-start.4
  614.4 2.8 multiply_add_fusion.1
  619.6 15.8 %all-to-all-done.4 = bf16[8,64,2,704]{3,2,1,0:T(2,128)(2,1)} async-done(((bf16[8,64,2,704]{3,2,1,0:T(2,128)(2,1)}), bf16[8,64,2,704]{3,2,1,0:T(2,128)(2,1)}, u32[]{:S(2)}, u32[]{:S(2)}) %all-to-all-start.4) | async-done | bytes 1441824 | tf_op jit(solution)/shard_map/all_to_all | solution.py:510
  639.7 2.6 concatenate.113
  651.6 6.3 multiply_subtract_fusion
  659.2 4.1 pad_maximum_fusion
  (320 shorter events, 122.4 us)
Async XLA Ops:
  7.2 146.5 %all-gather.7.cloned.1.call-start = ((), (), s32[]{:S(2)}) async-start(), calls=%async_computation.11 | async-start | bytes 1310720 | tf_op jit(solution)/shard_map/all_gather | solution.py:445
  9.7 146.5 %all-gather.5.cloned.1.call-start = ((), (), s32[]{:S(2)}) async-start(), calls=%async_computation.10 | async-start | bytes 3932160 | tf_op jit(solution)/shard_map/all_gather | solution.py:448
  29.0 210.8 %all-gather.9.cloned.1.call-start = ((), (), s32[]{:S(2)}) async-start(), calls=%async_computation.12 | async-start | bytes 7208960 | tf_op jit(solution)/shard_map/all_gather | solution.py:452
  69.1 8.1 %copy-start.17 = (f32[1,128,2048]{2,1,0:T(8,128)S(1)}, f32[1,128,2048]{2,1,0:T(8,128)}, u32[]{:S(2)}) copy-start(f32[1,128,2048]{2,1,0:T(8,128)} %param.13) | copy-start | bytes 3145732
  70.1 7.7 %copy-start.38 = (f32[7,64]{1,0:T(8,128)S(1)}, f32[7,64]{1,0:T(8,128)}, u32[]{:S(2)}) copy-start(f32[7,64]{1,0:T(8,128)} %param.17) | copy-start | bytes 5380
  70.1 7.7 %copy-start.26 = (s32[1,1024]{1,0:T(1,128)S(1)}, s32[1,1024]{1,0:T(1,128)}, u32[]{:S(2)}) copy-start(s32[1,1024]{1,0:T(1,128)} %param.14) | copy-start | bytes 12292
  73.0 80.4 %all-to-all-start.2 = ((bf16[8,64,704]{2,1,0:T(8,128)(2,1)}), bf16[8,64,704]{2,1,0:T(8,128)(2,1)}, u32[]{:S(2)}, u32[]{:S(2)}) async-start(bf16[8,64,704]{2,1,0:T(8,128)(2,1)} %bitcast.231), calls=%async_computation.2 | async-start | bytes 1572864 | tf_op jit(solution)/shard_map/all_to_all | solution.py:439
  77.2 198.5 %all-gather.11.cloned.1.call-start = ((), (), s32[]{:S(2)}) async-start(), calls=%async_computation.13 | async-start | bytes 3932160 | tf_op jit(solution)/shard_map/all_gather | solution.py:450
  93.3 5.9 copy-start.34
  95.4 4.9 copy-start.6
  98.9 113.6 %copy-start.2 = (f32[128,2048]{1,0:T(8,128)}, f32[128,2048]{1,0:T(8,128)S(1)}, u32[]{:S(2)}) copy-start(f32[128,2048]{1,0:T(8,128)S(1)} %copy.130) | copy-start | bytes 3145732
  98.9 53.4 %copy-start.41 = (f32[128]{0:T(128)}, f32[128]{0:T(128)S(1)}, u32[]{:S(2)}) copy-start(f32[128]{0:T(128)S(1)} %broadcast_multiply_fusion.6) | copy-start | bytes 1540
  99.2 53.1 %copy-start.44 = (f32[128]{0:T(128)}, f32[128]{0:T(128)S(1)}, u32[]{:S(2)}) copy-start(f32[128]{0:T(128)S(1)} %add_rsqrt_fusion.1) | copy-start | bytes 1540
  153.4 10.2 %copy-start.32 = (f32[1024,8]{0,1:T(8,128)}, f32[1024,8]{0,1:T(8,128)S(1)}, u32[]{:S(2)}) copy-start(f32[1024,8]{0,1:T(8,128)S(1)} %get-tuple-element.322) | copy-start | bytes 98308
  153.4 303.2 %reduce-scatter.11.cloned.1.call-start = ((), (), s32[]{:S(2)}) async-start(), calls=%async_computation.17 | async-start | bytes 3604480 | tf_op jit(solution)/shard_map/reduce_scatter | solution.py:507
  187.6 2.7 copy-start.19
  275.6 12.1 %copy-start.15 = (bf16[8,128,2048]{2,1,0:T(8,128)(2,1)S(1)}, bf16[8,128,2048]{2,1,0:T(8,128)(2,1)}, u32[]{:S(2)}) copy-start(bf16[8,128,2048]{2,1,0:T(8,128)(2,1)} %plane_gather.6) | copy-start | bytes 12582916
  292.3 190.4 %reduce-scatter.5.cloned.1.call-start = ((), (), s32[]{:S(2)}) async-start(), calls=%async_computation.14 | async-start | bytes 3932160 | tf_op jit(solution)/shard_map/reduce_scatter | solution.py:507
  292.3 4.5 copy-start.16
  315.5 23.5 %copy-start.7 = (f32[128,2048]{1,0:T(8,128)S(1)}, f32[128,2048]{1,0:T(8,128)}, u32[]{:S(2)}) copy-start(f32[128,2048]{1,0:T(8,128)} %copy-done.6) | copy-start | bytes 3145732
  365.9 5.5 copy-start.1
  378.2 2.6 copy-start.31
  380.8 4.0 copy-start.28
  380.8 4.0 copy-start.22
  393.8 2.6 copy-start.31
  396.4 4.0 copy-start.28
  396.4 4.0 copy-start.22
  404.8 3.1 copy-start.14
  412.9 111.5 %reduce-scatter.7.cloned.1.call-start = ((), (), s32[]{:S(2)}) async-start(), calls=%async_computation.15 | async-start | bytes 1310720 | tf_op jit(solution)/shard_map/reduce_scatter | solution.py:507
  417.5 187.4 %reduce-scatter.9.cloned.1.call-start = ((), (), s32[]{:S(2)}) async-start(), calls=%async_computation.16 | async-start | bytes 7208960 | tf_op jit(solution)/shard_map/reduce_scatter | solution.py:507
  425.9 22.1 %copy-start.3 = (f32[128,2048]{1,0:T(8,128)S(1)}, f32[128,2048]{1,0:T(8,128)}, u32[]{:S(2)}) copy-start(f32[128,2048]{1,0:T(8,128)} %copy-done.2) | copy-start | bytes 3145732
  425.9 22.1 %copy-start.35 = (f32[2048]{0:T(1024)S(1)}, f32[2048]{0:T(1024)}, u32[]{:S(2)}) copy-start(f32[2048]{0:T(1024)} %copy-done.34) | copy-start | bytes 24580
  425.9 22.1 %copy-start.42 = (f32[128]{0:T(128)S(1)}, f32[128]{0:T(128)}, u32[]{:S(2)}) copy-start(f32[128]{0:T(128)} %copy-done.41) | copy-start | bytes 1540
  425.9 22.1 %copy-start.45 = (f32[128]{0:T(128)S(1)}, f32[128]{0:T(128)}, u32[]{:S(2)}) copy-start(f32[128]{0:T(128)} %copy-done.44) | copy-start | bytes 1540
  458.9 27.3 %all-to-all-start.5 = ((bf16[8,64,1,704]{3,1,2,0:T(8,128)(2,1)}), bf16[8,64,1,704]{3,1,2,0:T(8,128)(2,1)}, u32[]{:S(2)}, u32[]{:S(2)}) async-start(bf16[8,64,1,704]{3,1,2,0:T(8,128)(2,1)} %bitcast.314), calls=%async_computation.9 | async-start | bytes 1572864 | tf_op jit(solution)/shard_map/all_to_all | solution.py:510
  480.0 10.9 %copy-start.37 = (f32[8,256]{1,0:T(8,128)S(1)}, f32[8,256]{1,0:T(8,128)}, u32[]{:S(2)}) copy-start(f32[8,256]{1,0:T(8,128)} %vector_sum.1) | copy-start | bytes 24580
  486.2 47.0 %all-to-all-start.3 = ((bf16[8,64,3,256]{3,1,2,0:T(8,128)(2,1)}), bf16[8,64,3,256]{3,1,2,0:T(8,128)(2,1)}, u32[]{:S(2)}, u32[]{:S(2)}) async-start(bf16[8,64,3,256]{3,1,2,0:T(8,128)(2,1)} %copy.147), calls=%async_computation.4 | async-start | bytes 1572864 | tf_op jit(solution)/shard_map/all_to_all | solution.py:510
  490.9 32.2 %copy-start.40 = (f32[7,64]{1,0:T(8,128)}, f32[7,64]{1,0:T(8,128)S(1)}, u32[]{:S(2)}) copy-start(f32[7,64]{1,0:T(8,128)S(1)} %get-tuple-element.282) | copy-start | bytes 5380
  520.1 3.1 copy-start.39
  537.3 3.0 copy-start.4
  537.3 3.7 copy-start.9
  610.1 25.3 %all-to-all-start.4 = ((bf16[8,64,2,704]{3,2,1,0:T(2,128)(2,1)}), bf16[8,64,2,704]{3,2,1,0:T(2,128)(2,1)}, u32[]{:S(2)}, u32[]{:S(2)}) async-start(bf16[8,64,2,704]{3,2,1,0:T(2,128)(2,1)} %reshape.683), calls=%async_computation.7 | async-start | bytes 3145728 | tf_op jit(solution)/shard_map/all_to_all | solution.py:510
  642.4 7.6 %slice-start = ((s8[8650752]{0:T(1024)(128)(4,1)}), s8[262144]{0:T(1024)(128)(4,1)S(1)}, s32[]{:S(2)}) async-start(s8[8650752]{0:T(1024)(128)(4,1)} %bitcast.273), calls=%async_computation.18 | async-start | bytes 524288
  645.0 4.8 copy-start.13
  645.0 5.0 slice-start.1
  647.1 2.7 copy-start.12
  647.1 4.4 slice-start.2
  649.9 8.0 %copy-start.5 = (f32[64,16896]{1,0:T(8,128)}, f32[64,16896]{1,0:T(8,128)S(1)}, u32[]{:S(2)}) copy-start(f32[64,16896]{1,0:T(8,128)S(1)} %constant_dynamic-update-slice_fusion.2) | copy-start | bytes 12976132
  (21 other events, 29.2 us)
Sparse Core Ops, SparseCore 0:
  10.1 30.6 all-gather.6
  42.4 63.1 all-gather.4
  107.2 105.2 all-gather.8
  213.9 61.6 all-gather.10
  292.4 54.9 reduce-scatter.10
  413.0 58.2 reduce-scatter.4
  474.1 27.1 reduce-scatter.6
  504.2 100.7 reduce-scatter.8

commit v3 on v2

--- a/solution.py
+++ b/solution.py
@@ -91,13 +91,67 @@
     return (col_ids[None, :] <= row_ids[:, None]) & (segment_ids[None, :] == row_segments[:, None])
 
 
-def adamw_update(weight, grad, moments, decay):
-    first = beta_first * moments[0] + (1.0 - beta_first) * grad
-    second = beta_second * moments[1] + (1.0 - beta_second) * grad * grad
+def adamw_terms(weight, grad, first_moment, second_moment, decay):
+    first = beta_first * first_moment + (1.0 - beta_first) * grad
+    second = beta_second * second_moment + (1.0 - beta_second) * grad * grad
     correct_one = 1.0 - beta_first**adam_step
     correct_two = 1.0 - beta_second**adam_step
     update = first / correct_one / (jnp.sqrt(second / correct_two) + adam_epsilon)
-    return (weight - learn_rate * (update + decay * weight), jnp.stack([first, second]))
+    return weight - learn_rate * (update + decay * weight), first, second
+
+
+def adamw_update(weight, grad, moments, decay):
+    new, first, second = adamw_terms(weight, grad, moments[0], moments[1], decay)
+    return new, jnp.stack([first, second])
+
+
+def adamw_kernel(places, chunk, w_ref, m_ref, *refs):
+    *piece_refs, g_ref, new_ref, state_ref = refs
+    for ref, moves in zip(piece_refs, places):
+        for index, source, target, width in moves:
+            values = ref[:, source : source + width] if index is None else ref[index, :, source : source + width]
+            g_ref[:, target : target + width] = values.astype(f32)
+
+    @pl.loop(0, g_ref.shape[1] // chunk)
+    def _(step):
+        cols = pl.ds(pl.multiple_of(step * chunk, chunk), chunk)
+        new, first, second = adamw_terms(
+            w_ref[:, cols], g_ref[:, cols], m_ref[0, :, cols], m_ref[1, :, cols], decay_rate
+        )
+        new_ref[:, cols] = new
+        state_ref[0, :, cols] = first
+        state_ref[1, :, cols] = second
+
+
+def adamw_pieces(weight, moments, pieces, places, chunk):
+    rows, cols = weight.shape
+    step = min(16, rows)
+    wide = pl.BlockSpec((step, cols), lambda i: (i, 0))
+    pair = pl.BlockSpec((2, step, cols), lambda i: (0, i, 0))
+    piece_specs = []
+    for piece in pieces:
+        if piece.ndim == 3:
+            piece_specs.append(
+                pl.BlockSpec((piece.shape[0], step, piece.shape[2]), lambda i: (0, i, 0))
+            )
+        else:
+            piece_specs.append(pl.BlockSpec((step, piece.shape[1]), lambda i: (i, 0)))
+    return pl.pallas_call(
+        lambda *refs: adamw_kernel(places, chunk, *refs),
+        grid=(rows // step,),
+        out_shape=(
+            jax.ShapeDtypeStruct((rows, cols), f32),
+            jax.ShapeDtypeStruct((rows, cols), f32),
+            jax.ShapeDtypeStruct((2, rows, cols), f32),
+        ),
+        in_specs=[wide, pair, *piece_specs],
+        out_specs=(wide, wide, pair),
+        compiler_params=pltpu.CompilerParams(vmem_limit_bytes=48 << 20),
+        cost_estimate=pl.CostEstimate(
+            flops=16 * rows * cols, bytes_accessed=30 * rows * cols, transcendentals=rows * cols
+        ),
+        name="adamw_pieces",
+    )(weight, moments, *pieces)
 
 
 def plane_places():
@@ -493,12 +547,13 @@
     hidden = inputs + scatter_tokens(jnp.dot(attended, out_weights, preferred_element_type=f32), 3)
     normed_two, normal_two, inverse_two = norm_forward(hidden, gain_two, shift_two)
     normed_two_all = gather_tokens(normed_two.astype(bf16), 4)
-    grad_act = jnp.dot(cotangent_all, down_weights, preferred_element_type=f32)
     gate_up = jnp.dot(normed_two_all, in_weights, preferred_element_type=f32)
     gate_part = gate_up[:, :unit_width]
     up_part = gate_up[:, unit_width:]
     sigmoid_gate = jax.nn.sigmoid(gate_part)
     activated = (gate_part * sigmoid_gate * up_part).astype(bf16)
+    down_term = contract_rows(cotangent_all, activated).astype(bf16)
+    grad_act = jnp.dot(after(cotangent_all, down_term), down_weights, preferred_element_type=f32)
     grad_gate = grad_act * up_part * sigmoid_gate * (1.0 + gate_part * (1.0 - sigmoid_gate))
     grad_up = grad_act * gate_part * sigmoid_gate
     grad_gate_up = jnp.concatenate([grad_gate, grad_up], axis=1).astype(bf16)
@@ -506,17 +561,17 @@
     def reduce_rows(term):
         return lax.psum_scatter(term, "fsdp", scatter_dimension=0, tiled=True)
 
-    def collect_rows(total, parts, width):
-        moved = lax.all_to_all(
-            total.reshape(groups, owned_rows, parts, width),
-            "seq",
-            split_axis=0,
-            concat_axis=0,
-            tiled=True,
-        ).astype(f32)
-        return moved.transpose(1, 2, 0, 3).reshape(owned_rows, parts * groups * width)
-
-    down_term = contract_rows(cotangent_all, activated).astype(bf16)
+    def collect_rows(total):
+        blocks = total.reshape(groups, owned_rows, total.shape[1])
+        return lax.all_to_all(blocks, "seq", split_axis=0, concat_axis=0, tiled=True)
+
+    def column_moves(parts, width, start):
+        return [
+            (group, part * width, start + part * groups * width + group * width, width)
+            for part in range(parts)
+            for group in range(groups)
+        ]
+
     down_sum = reduce_rows(down_term)
     in_term = contract_rows(normed_two_all, after(grad_gate_up, down_term)).astype(bf16)
     in_sum = reduce_rows(in_term)
@@ -597,19 +652,10 @@
     grad_normed_one = scatter_tokens(
         contract_cols(after(grad_projected_low, out_term), qkv_weights), 8
     )
-    result = hidden + scatter_tokens(
-        contract_cols(after(activated, grad_normed_one), down_weights), 7
-    )
     grad_stream = grad_hidden + norm_backward(grad_normed_one, normal_one, inverse_one, gain_one)
     grad_gain_one = jnp.sum(grad_normed_one * normal_one, axis=0)
     grad_shift_one = jnp.sum(grad_normed_one, axis=0)
 
-    feedforward_grad = jnp.concatenate(
-        [collect_rows(in_sum, 2, unit_width), collect_rows(down_sum, 1, unit_width)], axis=1
-    )
-    attention_grad = jnp.concatenate(
-        [collect_rows(qkv_sum, 3, local_width), from_order(out_sum.astype(f32))], axis=1
-    )
     bias_rows = lax.dynamic_update_slice_in_dim(
         jnp.zeros((3, D), f32), grad_bias.reshape(3, local_width), my_rank * local_width, axis=1
     )
@@ -621,11 +667,25 @@
         ]
     )
     vector_grad = sum_vectors(vector_term, 10)
-    attention_new, attention_state = adamw_update(
-        attention_weights, attention_grad, attention_moments, decay_rate
-    )
-    feedforward_new, feedforward_state = adamw_update(
-        feedforward_weights, feedforward_grad, feedforward_moments, decay_rate
+    result = hidden + scatter_tokens(
+        contract_cols(after(activated, vector_grad), down_weights), 7
+    )
+    in_moved = collect_rows(after(in_sum, vector_grad))
+    down_moved = collect_rows(down_sum)
+    qkv_moved = collect_rows(after(qkv_sum, result, in_moved))
+    feedforward_grad, feedforward_new, feedforward_state = adamw_pieces(
+        feedforward_weights,
+        feedforward_moments,
+        [after(in_moved, result), after(down_moved, result)],
+        [column_moves(2, unit_width, 0), column_moves(1, unit_width, 2 * FF)],
+        1408,
+    )
+    attention_grad, attention_new, attention_state = adamw_pieces(
+        attention_weights,
+        attention_moments,
+        [after(qkv_moved, feedforward_grad), from_order(after(out_sum, feedforward_grad))],
+        [column_moves(3, local_width, 0), [(None, 0, 3 * D, D)]],
+        1024,
     )
     vector_new, vector_state = adamw_update(norm_vectors, vector_grad, vector_moments, 0.0)
     return (

time: 680 us -> 577 us (0.85)
  waiting for transfers between devices: 102 us -> 39.4 us
  local copies, waits for them, and re-layouts: 87.9 us -> 61.2 us
  other arithmetic: 58.3 us -> 38 us
  Pallas kernels: 226 us -> 238 us
    reduce_scatter x4, waiting for transfers between devices: 61.1 us -> 10.9 us  [reduce_rows(): return lax.psum_scatter(term, 'fsdp', scatter_dimension=0, tiled=True)]
    pallas_call x0 -> x2, Pallas kernels: none -> 19.4 us  [adamw_pieces(): pl.pallas_call(lambda *refs: adamw_kernel(places, chunk, *refs), grid=(ro...]
    reshape x5 -> x0, local copies, waits for them, and re-layouts: 13 us -> none  [the longest x3 8.7 us: collect_rows(): total.reshape(groups, owned_rows, parts, width)]
    all_gather x1, waiting for transfers between devices: 24 us -> 13.7 us  [body(): down_weights = lax.all_gather(down_block, 'fsdp', axis=0, tiled=True)]
    sub x2 -> x0, other arithmetic: 9.16 us -> none  [adamw_update(): weight - learn_rate * (update + decay * weight)]
    unnamed x98 -> x85, local copies, waits for them, and re-layouts: 24.6 us -> 15.9 us
  transfers between devices with their start and end apart: 12 -> 12, of which waited for: 3 -> 5; matrix products, arithmetic and copies ran while one was open for 29% -> 32% of each run, Pallas kernels for 34% -> 41%
where the time goes in v3:
time: 577 us; the launch traced here: 567 us
  Pallas kernels  238 us (41%)
  matrix products  109 us (19%)
  local copies, waits for them, and re-layouts  61.2 us (11%)
  blocking collectives  41.5 us (7%)
  waiting for transfers between devices  39.4 us (7%)
  other arithmetic  38 us (7%)
  starting transfers between devices  16.4 us (3%)
  between operations  15.7 us (3%)
  loops' own time  8.33 us (1%)
    pallas_call x4, Pallas kernels, plane_gather(): pl.pallas_call(gather_kernel, out_shape=jax.ShapeDtypeStruct((8, rows, co...  103 us
    pallas_call x4, Pallas kernels, plane_scatter(): pl.pallas_call(scatter_kernel, out_shape=jax.ShapeDtypeStruct((rows, cols...  90.8 us
    all_to_all x2, blocking collectives, spread_columns(): lax.all_to_all(blocks, 'seq', split_axis=0, concat_axis=0, tiled=True)  41.5 us
    dot_general x4, matrix products, contract_cols(): lax.dot_general(left, right, (((1,), (1,)), ((), ())), preferred_element_...  25 us
    dot_general x4, matrix products, contract_rows(): lax.dot_general(left, right, (((0,), (0,)), ((), ())), preferred_element_...  23.2 us
    pallas_call x2, Pallas kernels, adamw_pieces(): pl.pallas_call(lambda *refs: adamw_kernel(places, chunk, *refs), grid=(ro...  19.4 us
    unnamed x85, local copies, waits for them, and re-layouts  15.9 us
    all_to_all x3, waiting for transfers between devices, collect_rows(): lax.all_to_all(blocks, 'seq', split_axis=0, concat_axis=0, tiled=True)  13.8 us
  transfers between devices with their start and end apart: 12, of which 5 were waited for; matrix products, arithmetic and copies ran while one was open for 32% of the time, Pallas kernels for 41%

profile of v3, /device:TPU:0, one launch (start us, length us, event | category | flops | bytes accessed | tf_op | source)
XLA Modules:
  0.0 567.4 jit_solution(6854662069880253436)
XLA Ops:
  11.3 17.6 %all_to_all.30 = bf16[8,64,768]{2,1,0:T(8,128)(2,1)} all-to-all(bf16[8,64,768]{2,1,0:T(8,128)(2,1)S(1)} %reshape.455), channel_id=1, replica_groups=mesh['seq'=8,'fsdp'=4] {'seq'}, dimensions={0} | all-to-all | bytes 1572864 | tf_op jit(solution)/shard_map/all_to_all | solution.py:493
  32.7 4.2 reshape.463
  36.9 3.8 copy.133
  40.6 4.6 reshape.464
  45.3 23.9 %all_to_all.31 = bf16[8,64,1408]{2,1,0:T(8,128)(2,1)} all-to-all(bf16[8,64,1408]{2,1,0:T(8,128)(2,1)} %reshape.464), channel_id=1, replica_groups=mesh['seq'=8,'fsdp'=4] {'seq'}, dimensions={0} | all-to-all | bytes 2883584 | tf_op jit(solution)/shard_map/all_to_all | solution.py:493
  71.0 3.5 all-to-all-start.2
  77.5 13.7 %vector_gather.1 = f32[8,4,8,128]{3,2,1,0:T(8,128)} custom-call(f32[8,128]{1,0:T(8,128)} %pad_convert_fusion.x_ref), custom_call_target="tpu_custom_call" | custom-call | tf_op jit(solution)/shard_map/vector_gather/pallas_call | solution.py:400
  102.2 25.8 %plane_gather.4 = bf16[8,128,2048]{2,1,0:T(8,128)(2,1)} custom-call(bf16[128,2048]{1,0:T(8,128)(2,1)} %add_convert_fusion.1.x_ref), custom_call_target="tpu_custom_call" | custom-call | tf_op jit(solution)/shard_map/plane_gather/pallas_call | solution.py:220
  128.0 26.0 %plane_gather.6 = bf16[8,128,2048]{2,1,0:T(8,128)(2,1)} custom-call(bf16[128,2048]{1,0:T(8,128)(2,1)} %convert_element_type.128.x_ref), custom_call_target="tpu_custom_call" | custom-call | tf_op jit(solution)/shard_map/plane_gather/pallas_call | solution.py:220
  158.7 6.3 %convolution_add_fusion = f32[1024,768]{0,1:T(8,128)S(1)} fusion(bf16[1024,2048]{1,0:T(8,128)(2,1)} %bitcast.241, bf16[2048,768]{1,0:T(8,128)(2,1)} %all-gather.5.cloned.1.call-done, f32[768]{0:T(1024)S(1)} %add.173), kind=kOutput, calls=%fused_computation.63 | convolution fusion | flops 3222011904 | bytes 10488832 | tf_op jit(solution)/shard_map/dot_general | solution.py:522
  165.6 22.4 %while.27 = (s32[]{:T(128)}, bf16[2,512,4,64]{1,3,2,0:T(8,128)(2,1)S(1)}, f32[2,4,512]{2,1,0:T(4,128)S(1)}, s32[2]{0:T(128)S(1)}, s32[1,1024]{1,0:T(1,128)S(1)},...) while((s32[]{:T(128)}, ...), condition=%wide.region_7.8_spmd, body=%wide.region_4.7_spmd.sunk | while | flops 563739136 | bytes 28915904 | solution.py:544
  173.7 3.1 fusion.110
  184.9 3.1 fusion.110
  188.6 2.7 convolution_convert_fusion.3
  191.4 22.1 %plane_scatter.4 = f32[128,2048]{1,0:T(8,128)S(1)} custom-call(bf16[8,128,2048]{2,1,0:T(8,128)(2,1)S(1)} %bitcast.224), custom_call_target="tpu_custom_call" | custom-call | tf_op jit(solution)/shard_map/plane_scatter/pallas_call | solution.py:290
  215.0 25.5 %plane_gather.5 = bf16[8,128,2048]{2,1,0:T(8,128)(2,1)} custom-call(bf16[128,2048]{1,0:T(8,128)(2,1)} %add_convert_fusion.x_ref), custom_call_target="tpu_custom_call" | custom-call | tf_op jit(solution)/shard_map/plane_gather/pallas_call | solution.py:220
  240.6 12.1 %fusion.52 = f32[1024,1408]{1,0:T(8,128)} fusion(bf16[1024,2048]{1,0:T(8,128)(2,1)} %bitcast.247, bf16[2048,1408]{1,0:T(8,128)(2,1)} %all-gather.9.cloned.1.call-done), kind=kOutput, calls=%fused_computation.145 | convolution fusion | flops 5905580032 | bytes 15728640 | tf_op jit(solution)/shard_map/dot_general | solution.py:550
  252.7 4.1 multiply_convert_fusion.3
  258.0 4.5 fusion.37
  262.5 13.7 %all-gather.11.cloned.1.call-done = bf16[2048,704]{1,0:T(8,128)(2,1)} async-done(((bf16[512,704]{1,0:T(8,128)(2,1)}), bf16[2048,704]{1,0:T(8,128)(2,1)}) %all-gather.11.cloned.1.call-update) | async-done | bytes 2883600 | tf_op jit(solution)/shard_map/all_gather | solution.py:504
  276.2 9.1 %multiply_convert_fusion.2 = (bf16[1024,704]{1,0:T(8,128)(2,1)S(1)}, bf16[1024,704]{1,0:T(8,128)(2,1)S(1)}) fusion(f32[1024,1408]{1,0:T(8,128)} %fusion.52, bf16[1024,2048]{1,0:T(8,128)(2,1)} %bitcast.245, bf16[2048,704]{1,0:T(8,128)(2,1)} %all-gather.11.cloned.1.call-done), kind=kOutput, calls=%fused_computation.55 | convolution fusion | flops 2962161664 | bytes 15728640 | tf_op jit(solution)/shard_map/dot_general | solution.py:556
  288.4 8.8 %convolution_convert_fusion.1 = bf16[2048,1408]{1,0:T(8,128)(2,1)} fusion(bf16[1024,2048]{1,0:T(8,128)(2,1)S(1)} %bitcast.248, bf16[1024,1408]{1,0:T(8,128)(2,1)S(1)} %pad_maximum_fusion.1), kind=kOutput, calls=%fused_computation.46 | convolution fusion | flops 5908463616 | bytes 12845056 | tf_op jit(solution)/shard_map/dot_general | solution.py:79
  299.3 9.7 %convolution_convert_fusion.2 = bf16[1024,2048]{1,0:T(8,128)(2,1)S(1)} fusion(bf16[1024,1408]{1,0:T(8,128)(2,1)} %copy-done.17, bf16[2048,1408]{1,0:T(8,128)(2,1)} %all-gather.9.cloned.1.call-done), kind=kOutput, calls=%fused_computation.47 | convolution fusion | flops 5907677184 | bytes 12845056 | tf_op jit(solution)/shard_map/dot_general | solution.py:83
  309.0 22.9 %plane_scatter.5 = f32[128,2048]{1,0:T(8,128)S(1)} custom-call(bf16[8,128,2048]{2,1,0:T(8,128)(2,1)S(1)} %bitcast.225), custom_call_target="tpu_custom_call" | custom-call | tf_op jit(solution)/shard_map/plane_scatter/pallas_call | solution.py:290
  334.0 25.4 %plane_gather.7 = bf16[8,128,2048]{2,1,0:T(8,128)(2,1)} custom-call(bf16[128,2048]{1,0:T(8,128)(2,1)} %get-tuple-element.298.x_ref), custom_call_target="tpu_custom_call" | custom-call | tf_op jit(solution)/shard_map/plane_gather/pallas_call | solution.py:220
  359.4 3.8 convolution_convert_fusion.9
  364.1 29.4 %while.28 = (s32[]{:T(128)}, f32[1024,4,64]{0,2,1:T(8,128)S(1)}, f32[1024,4,64]{0,2,1:T(8,128)}, bf16[2,512,4,64]{1,3,2,0:T(8,128)(2,1)}, s32[2]{0:T(128)S(1)}, ...) while((s32[]{:T(128)}, f32[1024,4,64]{0,2,1:T(8,128)S(1)}, ...), condition=%wide.region_14.15_spmd.clone, body=%wide.region_12.14_spmd.clone.sunk | while | flops 1368521216 | bytes 61667716 | solution.py:623
  369.8 2.6 fusion.124
  372.4 3.9 multiply_convert_fusion.5
  384.4 2.6 fusion.124
  387.0 3.9 multiply_convert_fusion.5
  398.2 5.1 convolution_convert_fusion.6
  404.5 4.8 convolution_convert_fusion.8
  409.2 5.6 convolution_convert_fusion.5
  414.9 22.1 %plane_scatter.6 = f32[128,2048]{1,0:T(8,128)S(1)} custom-call(bf16[8,128,2048]{2,1,0:T(8,128)(2,1)S(1)} %bitcast.226), custom_call_target="tpu_custom_call" | custom-call | tf_op jit(solution)/shard_map/plane_scatter/pallas_call | solution.py:290
  439.0 11.1 %vector_sum.1 = f32[8,256]{1,0:T(8,128)} custom-call(f32[8,8,256]{2,1,0:T(8,128)} %pad.12.x_ref), custom_call_target="tpu_custom_call" | custom-call | tf_op jit(solution)/shard_map/vector_sum/pallas_call | solution.py:416
  451.5 3.6 all-to-all-start.3
  455.8 2.7 reduce-scatter.9.cloned.1.call-done
  460.7 13.8 %all-to-all-done.3.refs_2_ = bf16[8,64,1408]{2,1,0:T(8,128)(2,1)S(1)} async-done(((bf16[8,64,1408]{2,1,0:T(8,128)(2,1)}), bf16[8,64,1408]{2,1,0:T(8,128)(2,1)S(1)}, u32[]{:S(2)}, u32[]{:S(2)}) %all-to-all-start.3) | async-done | bytes 1441824 | tf_op jit(solution)/shard_map/all_to_all | solution.py:566
  474.6 4.2 all-to-all-start.5
  478.8 5.8 %convolution_convert_fusion.4 = bf16[1024,2048]{1,0:T(8,128)(2,1)S(1)} fusion(bf16[1024,704]{1,0:T(8,128)(2,1)} %copy-done.23, bf16[2048,704]{1,0:T(8,128)(2,1)} %all-gather.11.cloned.1.call-done), kind=kOutput, calls=%fused_computation.49 | convolution fusion | flops 2954887168 | bytes 8519680 | tf_op jit(solution)/shard_map/dot_general | solution.py:83
  484.6 23.7 %plane_scatter.7 = f32[128,2048]{1,0:T(8,128)S(1)} custom-call(bf16[8,128,2048]{2,1,0:T(8,128)(2,1)S(1)} %bitcast.227), custom_call_target="tpu_custom_call" | custom-call | tf_op jit(solution)/shard_map/plane_scatter/pallas_call | solution.py:290
  509.5 2.6 copy.93
  514.4 7.1 %reduce-scatter.5.cloned.1.call-done = bf16[512,768]{1,0:T(8,128)(2,1)} async-done(((bf16[2048,768]{1,0:T(8,128)(2,1)}), bf16[512,768]{1,0:T(8,128)(2,1)}) %reduce-scatter.5.cloned.1.call-update) | async-done | bytes 786448 | tf_op jit(solution)/shard_map/reduce_scatter | solution.py:562
  521.5 4.5 all-to-all-start.4
  526.0 2.7 multiply_add_fusion
  537.4 12.5 %adamw_pieces.2 = (f32[64,16896]{1,0:T(8,128)}, f32[64,16896]{1,0:T(8,128)}, f32[2,64,16896]{2,1,0:T(8,128)}) custom-call(f32[64,16896]{1,0:T(8,128)} %refs_0_.2, f32[2,64,16896]{2,1,0:T(8,128)} %refs_1_.2, bf16[8,64,1408]{2,1,0:T(8,128)(2,1)S(1)} %all-to-all-done.3.refs_2_, bf16[8,64,704]{2,1,0:T(8,128)(2,1)} %all-to-all-done.5.refs_3_), custom_call_target="tpu_custom_call" | custom-call | flops 17301504 | bytes 32440320 | tf_op jit(solution)/shard_map/adamw_pieces/pallas_call | solution.py:139
  553.2 6.9 %adamw_pieces.3 = (f32[64,8192]{1,0:T(8,128)}, f32[64,8192]{1,0:T(8,128)}, f32[2,64,8192]{2,1,0:T(8,128)}) custom-call(f32[64,8192]{1,0:T(8,128)S(1)} %copy-done, f32[2,64,8192]{2,1,0:T(8,128)} %refs_1_.3, bf16[8,64,768]{2,1,0:T(8,128)(2,1)} %all-to-all-done.4.refs_2_, bf16[64,2048]{1,0:T(8,128)(2,1)S(1)} %reshape.488.refs_3_), custom_call_target="tpu_custom_call" | custom-call | flops 8388608 | bytes 15728640 | tf_op jit(solution)/shard_map/adamw_pieces/pallas_call | solution.py:139
  (276 shorter events, 91.4 us)
Async XLA Ops:
  7.2 149.0 %all-gather.7.cloned.1.call-start = ((), (), s32[]{:S(2)}) async-start(), calls=%async_computation.11 | async-start | bytes 1310720 | tf_op jit(solution)/shard_map/all_gather | solution.py:499
  9.7 149.1 %all-gather.5.cloned.1.call-start = ((), (), s32[]{:S(2)}) async-start(), calls=%async_computation.10 | async-start | bytes 3932160 | tf_op jit(solution)/shard_map/all_gather | solution.py:502
  29.0 211.6 %all-gather.9.cloned.1.call-start = ((), (), s32[]{:S(2)}) async-start(), calls=%async_computation.12 | async-start | bytes 7208960 | tf_op jit(solution)/shard_map/all_gather | solution.py:506
  69.3 6.9 %copy-start.13 = (f32[1,128,2048]{2,1,0:T(8,128)S(1)}, f32[1,128,2048]{2,1,0:T(8,128)}, u32[]{:S(2)}) copy-start(f32[1,128,2048]{2,1,0:T(8,128)} %param.13) | copy-start | bytes 3145732
  69.3 7.0 %copy-start.35 = (f32[7,64]{1,0:T(8,128)S(1)}, f32[7,64]{1,0:T(8,128)}, u32[]{:S(2)}) copy-start(f32[7,64]{1,0:T(8,128)} %param.17) | copy-start | bytes 5380
  69.3 7.0 %copy-start.24 = (s32[1,1024]{1,0:T(1,128)S(1)}, s32[1,1024]{1,0:T(1,128)}, u32[]{:S(2)}) copy-start(s32[1,1024]{1,0:T(1,128)} %param.14) | copy-start | bytes 12292
  71.0 84.0 %all-to-all-start.2 = ((bf16[8,64,704]{2,1,0:T(8,128)(2,1)}), bf16[8,64,704]{2,1,0:T(8,128)(2,1)S(1)}, u32[]{:S(2)}, u32[]{:S(2)}) async-start(bf16[8,64,704]{2,1,0:T(8,128)(2,1)} %bitcast.185), calls=%async_computation.2 | async-start | bytes 1572864 | tf_op jit(solution)/shard_map/all_to_all | solution.py:493
  74.5 201.6 %all-gather.11.cloned.1.call-start = ((), (), s32[]{:S(2)}) async-start(), calls=%async_computation.13 | async-start | bytes 3932160 | tf_op jit(solution)/shard_map/all_gather | solution.py:504
  92.7 8.1 %copy-start.32 = (f32[2048]{0:T(1024)}, f32[2048]{0:T(1024)S(1)}, u32[]{:S(2)}) copy-start(f32[2048]{0:T(1024)S(1)} %mul.329) | copy-start | bytes 24580
  96.9 2.0 copy-start.6
  100.4 113.1 %copy-start.3 = (f32[128,2048]{1,0:T(8,128)}, f32[128,2048]{1,0:T(8,128)S(1)}, u32[]{:S(2)}) copy-start(f32[128,2048]{1,0:T(8,128)S(1)} %copy.78) | copy-start | bytes 3145732
  101.1 52.8 %copy-start.42 = (f32[128]{0:T(128)}, f32[128]{0:T(128)S(1)}, u32[]{:S(2)}) copy-start(f32[128]{0:T(128)S(1)} %add_rsqrt_fusion.1) | copy-start | bytes 1540
  155.0 10.3 %copy-start.30 = (f32[1024,8]{0,1:T(8,128)}, f32[1024,8]{0,1:T(8,128)S(1)}, u32[]{:S(2)}) copy-start(f32[1024,8]{0,1:T(8,128)S(1)} %get-tuple-element.332) | copy-start | bytes 98308
  155.9 295.5 %reduce-scatter.7.cloned.1.call-start = ((), (), s32[]{:S(2)}) async-start(), calls=%async_computation.15 | async-start | bytes 7208960 | tf_op jit(solution)/shard_map/reduce_scatter | solution.py:562
  188.0 3.4 copy-start.9
  188.0 3.4 copy-start.28
  188.6 2.8 copy-start.15
  213.7 118.7 %copy-start.1 = (f32[128,2048]{1,0:T(8,128)}, f32[128,2048]{1,0:T(8,128)S(1)}, u32[]{:S(2)}) copy-start(f32[128,2048]{1,0:T(8,128)S(1)} %get-tuple-element.301) | copy-start | bytes 3145732
  252.7 5.3 copy-start.11
  285.3 3.1 copy-start.12
  297.2 161.2 %reduce-scatter.9.cloned.1.call-start = ((), (), s32[]{:S(2)}) async-start(), calls=%async_computation.16 | async-start | bytes 3604480 | tf_op jit(solution)/shard_map/reduce_scatter | solution.py:562
  299.2 222.2 %reduce-scatter.5.cloned.1.call-start = ((), (), s32[]{:S(2)}) async-start(), calls=%async_computation.14 | async-start | bytes 3932160 | tf_op jit(solution)/shard_map/reduce_scatter | solution.py:562
  309.0 23.4 %copy-start.7 = (f32[128,2048]{1,0:T(8,128)S(1)}, f32[128,2048]{1,0:T(8,128)}, u32[]{:S(2)}) copy-start(f32[128,2048]{1,0:T(8,128)} %copy-done.6) | copy-start | bytes 3145732
  359.4 4.7 copy-start.8
  369.8 2.6 copy-start.29
  372.4 4.0 copy-start.26
  372.4 4.0 copy-start.18
  384.4 2.6 copy-start.29
  387.0 4.0 copy-start.26
  387.0 4.0 copy-start.18
  395.4 2.8 copy-start.10
  398.2 5.2 copy-start.41
  404.4 4.8 copy-start.22
  414.9 22.1 %copy-start.4 = (f32[128,2048]{1,0:T(8,128)S(1)}, f32[128,2048]{1,0:T(8,128)}, u32[]{:S(2)}) copy-start(f32[128,2048]{1,0:T(8,128)} %copy-done.3) | copy-start | bytes 3145732
  414.9 22.1 %copy-start.33 = (f32[2048]{0:T(1024)S(1)}, f32[2048]{0:T(1024)}, u32[]{:S(2)}) copy-start(f32[2048]{0:T(1024)} %copy-done.32) | copy-start | bytes 24580
  414.9 22.1 %copy-start.40 = (f32[128]{0:T(128)S(1)}, f32[128]{0:T(128)}, u32[]{:S(2)}) copy-start(f32[128]{0:T(128)} %copy-done.39) | copy-start | bytes 1540
  414.9 22.1 %copy-start.43 = (f32[128]{0:T(128)S(1)}, f32[128]{0:T(128)}, u32[]{:S(2)}) copy-start(f32[128]{0:T(128)} %copy-done.42) | copy-start | bytes 1540
  451.4 82.6 %copy-start.37 = (f32[7,64]{1,0:T(8,128)}, f32[7,64]{1,0:T(8,128)S(1)}, u32[]{:S(2)}) copy-start(f32[7,64]{1,0:T(8,128)S(1)} %get-tuple-element.297) | copy-start | bytes 5380
  451.5 23.1 %all-to-all-start.3 = ((bf16[8,64,1408]{2,1,0:T(8,128)(2,1)}), bf16[8,64,1408]{2,1,0:T(8,128)(2,1)S(1)}, u32[]{:S(2)}, u32[]{:S(2)}) async-start(bf16[8,64,1408]{2,1,0:T(8,128)(2,1)} %bitcast.271), calls=%async_computation.5 | async-start | bytes 2883584 | tf_op jit(solution)/shard_map/all_to_all | solution.py:566
  455.0 96.0 %reduce-scatter.11.cloned.1.call-start = ((), (), s32[]{:S(2)}) async-start(), calls=%async_computation.17 | async-start | bytes 1310720 | tf_op jit(solution)/shard_map/reduce_scatter | solution.py:562
  474.6 46.9 %all-to-all-start.5 = ((bf16[8,64,704]{2,1,0:T(8,128)(2,1)}), bf16[8,64,704]{2,1,0:T(8,128)(2,1)}, u32[]{:S(2)}, u32[]{:S(2)}) async-start(bf16[8,64,704]{2,1,0:T(8,128)(2,1)} %bitcast.56), calls=%async_computation.8 | async-start | bytes 1572864 | tf_op jit(solution)/shard_map/all_to_all | solution.py:566
  484.6 23.8 %copy-start.2 = (f32[128,2048]{1,0:T(8,128)S(1)}, f32[128,2048]{1,0:T(8,128)}, u32[]{:S(2)}) copy-start(f32[128,2048]{1,0:T(8,128)} %copy-done.1) | copy-start | bytes 3145732
  509.5 16.5 %copy-start.5 = (f32[128,2048]{1,0:T(8,128)S(1)}, f32[128,2048]{1,0:T(8,128)}, u32[]{:S(2)}) copy-start(f32[128,2048]{1,0:T(8,128)} %copy-done.3) | copy-start | bytes 3145732
  521.5 31.7 %all-to-all-start.4 = ((bf16[8,64,768]{2,1,0:T(8,128)(2,1)}), bf16[8,64,768]{2,1,0:T(8,128)(2,1)}, u32[]{:S(2)}, u32[]{:S(2)}) async-start(bf16[8,64,768]{2,1,0:T(8,128)(2,1)} %bitcast.276), calls=%async_computation.6 | async-start | bytes 1572864 | tf_op jit(solution)/shard_map/all_to_all | solution.py:566
  528.7 5.4 copy-start.36
  528.7 6.7 %copy-start.38 = (f32[1,7,64]{2,1,0:T(8,128)S(1)}, f32[1,7,64]{2,1,0:T(8,128)}, u32[]{:S(2)}) copy-start(f32[1,7,64]{2,1,0:T(8,128)} %get-tuple-element.296) | copy-start | bytes 5380
  528.7 7.3 %copy-start.14 = (f32[128,2048]{0,1:T(8,128)S(1)}, f32[128,2048]{0,1:T(8,128)}, u32[]{:S(2)}) copy-start(f32[128,2048]{0,1:T(8,128)} %copy.93) | copy-start | bytes 3145732
  537.4 15.8 %copy-start = (f32[64,8192]{1,0:T(8,128)S(1)}, f32[64,8192]{1,0:T(8,128)}, u32[]{:S(2)}) copy-start(f32[64,8192]{1,0:T(8,128)} %refs_0_.3) | copy-start | bytes 6291460
  (13 other events, 14.5 us)
Sparse Core Ops, SparseCore 0:
  10.1 30.6 all-gather.6
  42.4 63.1 all-gather.4
  107.2 105.2 all-gather.8
  214.4 61.6 all-gather.10
  297.3 100.9 reduce-scatter.6
  401.0 57.3 reduce-scatter.8
  461.3 60.1 reduce-scatter.4
  523.8 27.1 reduce-scatter.10
